TPU v7x, 128 devices: a whole 4x4x4 slice. The times are simulated.
128 devices in a mesh: dp: 1, tp: 2 (over core), cp: 64 (over z, y, x).
Axes of the slice: x: 4, y: 4, z: 4, core: 2. Of those that a mesh axis runs over, the one named last changes fastest.
Arguments:
- tokens_in: bfloat16 [16384, 1536], P(('dp', 'cp', 'tp'))
- grad_out: bfloat16 [16384, 1536], P(('dp', 'cp', 'tp'))
- w_query: bfloat16 [1536, 1536], P(None, 'tp')
- w_key: bfloat16 [1536, 256], P(None, 'tp')
- w_value: bfloat16 [1536, 256], P(None, 'tp')
- w_out: bfloat16 [1536, 1536], P('tp')
Outputs:
- output 1: bfloat16 [16384, 1536], P(('dp', 'cp', 'tp'))
- output 2: bfloat16 [16384, 1536], P(('dp', 'cp', 'tp'))
All inputs are finite; a program needn't handle non-finite values.
Results may differ from a plain program's by a relative error of at most 0.00950505.
Values are sent between devices in bfloat16 or wider.
A program may use at most 1 GiB of HBM per device.

v0:
```python
import jax
import jax.numpy as jnp
from jax import lax
from jax.sharding import PartitionSpec as P

HEAD_DIM = 128


def block_rows(piece_rows, key_rows, head_count):
    budget = max(1, (1 << 22) // (key_rows * head_count))
    row_count = 8
    for candidate in (16, 32, 64, 128):
        if candidate <= budget and piece_rows % candidate == 0:
            row_count = candidate
    return row_count


def fold_positions(row_ids, seq_loc, cp_size):
    piece_rows = seq_loc // 2
    shard_idx = row_ids // seq_loc
    within = row_ids % seq_loc
    piece_id = jnp.where(within < piece_rows, shard_idx, 2 * cp_size - 1 - shard_idx)
    return piece_id * piece_rows + within % piece_rows


def dot_transposed(left, right):
    return lax.dot_general(left, right, (((1,), (1,)), ((), ())), preferred_element_type=jnp.float32)


def solution(mesh):
    cp_size = mesh.shape['cp']
    row_spec = P(('dp', 'cp', 'tp'), None)

    def local_step(x_blk, dy_blk, w_query, w_key, w_value, w_out):
        cp_rank = lax.axis_index('cp')
        x_loc = lax.all_gather(x_blk, 'tp', axis=0, tiled=True)
        seq_loc = x_loc.shape[0]
        seq_all = seq_loc * cp_size
        piece_rows = seq_loc // 2
        heads_q = w_query.shape[1] // HEAD_DIM
        heads_kv = w_key.shape[1] // HEAD_DIM
        group_size = heads_q // heads_kv
        score_scale = HEAD_DIM ** -0.5
        query_loc = jnp.dot(x_loc, w_query, preferred_element_type=jnp.float32).astype(jnp.bfloat16).reshape(seq_loc, heads_kv, group_size, HEAD_DIM)
        keys_loc = jnp.dot(x_loc, w_key, preferred_element_type=jnp.float32).astype(jnp.bfloat16).reshape(seq_loc, heads_kv, HEAD_DIM)
        values_loc = jnp.dot(x_loc, w_value, preferred_element_type=jnp.float32).astype(jnp.bfloat16).reshape(seq_loc, heads_kv, HEAD_DIM)
        keys_all = lax.all_gather(keys_loc, 'cp', axis=0, tiled=True)
        values_all = lax.all_gather(values_loc, 'cp', axis=0, tiled=True)
        dy_loc = lax.all_gather(dy_blk, 'tp', axis=0, tiled=True)
        d_out = dot_transposed(dy_loc, w_out).astype(jnp.bfloat16).reshape(seq_loc, heads_kv, group_size, HEAD_DIM)
        key_pos = fold_positions(jnp.arange(seq_all, dtype=jnp.int32), seq_loc, cp_size)
        query_pos = fold_positions(cp_rank * seq_loc + jnp.arange(seq_loc, dtype=jnp.int32), seq_loc, cp_size)
        blk_rows = block_rows(piece_rows, seq_all, heads_q)
        block_count = seq_loc // blk_rows

        def block_step(acc_pair, blk_in):
            dk_acc, dv_acc = acc_pair
            q_blk, do_blk, pos_blk = blk_in
            scores = jnp.einsum('qhgd,khd->hgqk', q_blk, keys_all, preferred_element_type=jnp.float32) * score_scale
            allowed = pos_blk[:, None] >= key_pos[None, :]
            scores = jnp.where(allowed, scores, -jnp.inf)
            log_norm = jax.nn.logsumexp(scores, axis=-1, keepdims=True)
            prob_bf = jnp.exp(scores - log_norm).astype(jnp.bfloat16)
            out_blk = jnp.einsum('hgqk,khd->qhgd', prob_bf, values_all, preferred_element_type=jnp.float32).astype(jnp.bfloat16)
            row_delta = jnp.einsum('qhgd,qhgd->hgq', do_blk, out_blk, preferred_element_type=jnp.float32)
            d_prob = jnp.einsum('qhgd,khd->hgqk', do_blk, values_all, preferred_element_type=jnp.float32)
            d_score = (prob_bf.astype(jnp.float32) * (d_prob - row_delta[..., None])).astype(jnp.bfloat16)
            dq_blk = (jnp.einsum('hgqk,khd->qhgd', d_score, keys_all, preferred_element_type=jnp.float32) * score_scale).astype(jnp.bfloat16)
            dk_acc = dk_acc + jnp.einsum('hgqk,qhgd->khd', d_score, q_blk, preferred_element_type=jnp.float32) * score_scale
            dv_acc = dv_acc + jnp.einsum('hgqk,qhgd->khd', prob_bf, do_blk, preferred_element_type=jnp.float32)
            return (dk_acc, dv_acc), (out_blk, dq_blk)

        zeros_kv = jnp.zeros((seq_all, heads_kv, HEAD_DIM), jnp.float32)
        blk_inputs = (query_loc.reshape(block_count, blk_rows, heads_kv, group_size, HEAD_DIM), d_out.reshape(block_count, blk_rows, heads_kv, group_size, HEAD_DIM), query_pos.reshape(block_count, blk_rows))
        (dk_part, dv_part), (out_blocks, dq_blocks) = lax.scan(block_step, (zeros_kv, zeros_kv), blk_inputs)
        attn_out = out_blocks.reshape(seq_loc, heads_q * HEAD_DIM)
        d_query = dq_blocks.reshape(seq_loc, heads_q * HEAD_DIM)
        y_part = jnp.dot(attn_out, w_out, preferred_element_type=jnp.float32)
        y_blk = lax.psum_scatter(y_part, 'tp', scatter_dimension=0, tiled=True).astype(jnp.bfloat16)
        dk_own = lax.psum_scatter(dk_part, 'cp', scatter_dimension=0, tiled=True).astype(jnp.bfloat16).reshape(seq_loc, heads_kv * HEAD_DIM)
        dv_own = lax.psum_scatter(dv_part, 'cp', scatter_dimension=0, tiled=True).astype(jnp.bfloat16).reshape(seq_loc, heads_kv * HEAD_DIM)
        dx_part = dot_transposed(d_query, w_query) + dot_transposed(dk_own, w_key) + dot_transposed(dv_own, w_value)
        dx_blk = lax.psum_scatter(dx_part, 'tp', scatter_dimension=0, tiled=True).astype(jnp.bfloat16)
        return y_blk, dx_blk

    return jax.shard_map(local_step, mesh=mesh, in_specs=(row_spec, row_spec, P(None, 'tp'), P(None, 'tp'), P(None, 'tp'), P('tp', None)), out_specs=(row_spec, row_spec), check_vma=False)
```

profile of v0, /device:TPU:1, one launch (start us, length us, event | category | flops | bytes accessed | tf_op | source)
XLA Modules:
  0.0 1290.2 jit_solution(11106991575633941656)
XLA Ops:
  24.1 57.4 %all-gather.7.cloned.1.call-done = bf16[16384,128]{1,0:T(8,128)(2,1)} async-done(((bf16[256,128]{1,0:T(8,128)(2,1)}), bf16[16384,128]{1,0:T(8,128)(2,1)}) %all-gather.7.cloned.1.call-update) | async-done | bytes 4194320 | tf_op jit(solution)/shard_map/all_gather | solution.py:48
  81.5 68.9 %all-gather.5.cloned.1.call-done = bf16[16384,128]{1,0:T(8,128)(2,1)} async-done(((bf16[256,128]{1,0:T(8,128)(2,1)}), bf16[16384,128]{1,0:T(8,128)(2,1)}) %all-gather.5.cloned.1.call-update) | async-done | bytes 4194320 | tf_op jit(solution)/shard_map/all_gather | solution.py:47
  150.4 369.3 %while.17 = (s32[]{:T(128)}, f32[16384,1,128]{0,2,1:T(8,128)}, f32[16384,1,128]{0,2,1:T(8,128)}, bf16[8,32,1,6,128]{4,1,3,2,0:T(8,128)(2,1)}, bf16[8,32,1,6,128]...) while((s32[]{:T(128)}, f32[16384,1,128]{0,2,1:T(8,128)}, ...), condition=%wide.region_3.4_spmd.clone, body=%wide.region_0.3_spmd.clone.sunk | while | flops 4878082560 | bytes 304669728 | solution.py:75
  159.1 9.1 exponential_convert_fusion.2
  168.3 4.9 fusion.120
  173.8 4.3 fusion.121
  180.5 6.3 fusion.122
  186.8 4.1 fusion.123
  203.0 9.1 exponential_convert_fusion.2
  212.1 4.9 fusion.120
  217.7 4.3 fusion.121
  224.4 8.9 fusion.122
  233.3 4.1 fusion.123
  241.1 3.9 fusion.119
  249.5 9.1 exponential_convert_fusion.2
  258.6 4.9 fusion.120
  264.1 4.3 fusion.121
  270.8 8.9 fusion.122
  279.8 4.1 fusion.123
  296.0 9.1 exponential_convert_fusion.2
  305.1 4.9 fusion.120
  310.6 4.3 fusion.121
  317.3 8.9 fusion.122
  326.3 4.1 fusion.123
  342.5 9.1 exponential_convert_fusion.2
  351.6 4.9 fusion.120
  357.1 4.3 fusion.121
  363.8 8.9 fusion.122
  372.8 4.1 fusion.123
  389.0 9.1 exponential_convert_fusion.2
  398.1 4.9 fusion.120
  403.6 4.3 fusion.121
  410.3 8.9 fusion.122
  419.3 4.1 fusion.123
  435.4 9.1 exponential_convert_fusion.2
  444.6 4.9 fusion.120
  450.1 4.3 fusion.121
  456.8 8.9 fusion.122
  465.7 4.1 fusion.123
  481.9 9.1 exponential_convert_fusion.2
  491.1 4.9 fusion.120
  496.6 4.3 fusion.121
  503.3 8.9 fusion.122
  512.2 4.1 fusion.123
  527.3 315.4 %reduce-scatter.7.cloned.1.call-done = f32[256,1,128]{0,2,1:T(8,128)} async-done(((f32[16384,1,128]{0,2,1:T(8,128)}), f32[256,1,128]{0,2,1:T(8,128)}) %reduce-scatter.7.cloned.1.call-update) | async-done | bytes 131088 | tf_op jit(solution)/shard_map/reduce_scatter | solution.py:80
  845.7 362.3 %reduce-scatter.9.cloned.1.call-done = f32[256,1,128]{0,2,1:T(8,128)} async-done(((f32[16384,1,128]{0,2,1:T(8,128)}), f32[256,1,128]{0,2,1:T(8,128)}) %reduce-scatter.9.cloned.1.call-update) | async-done | bytes 131088 | tf_op jit(solution)/shard_map/reduce_scatter | solution.py:81
  1211.1 55.3 %reduce-scatter.5.cloned.1.call-done = f32[128,1536]{1,0:T(8,128)} async-done(((f32[256,1536]{1,0:T(8,128)}), f32[128,1536]{1,0:T(8,128)}) %reduce-scatter.5.cloned.1.call-update) | async-done | bytes 786448 | tf_op jit(solution)/shard_map/reduce_scatter | solution.py:79
  1268.3 13.1 %reduce-scatter.11.cloned.1.call-done = f32[128,1536]{1,0:T(8,128)} async-done(((f32[256,1536]{1,0:T(8,128)}), f32[128,1536]{1,0:T(8,128)}) %reduce-scatter.11.cloned.1.call-update) | async-done | bytes 786448 | tf_op jit(solution)/shard_map/reduce_scatter | solution.py:83
  (266 shorter events, 151.2 us)
Async XLA Ops:
  7.2 13.0 %copy-start = (bf16[768,1536]{1,0:T(8,128)(2,1)S(1)}, bf16[768,1536]{1,0:T(8,128)(2,1)}, u32[]{:S(2)}) copy-start(bf16[768,1536]{1,0:T(8,128)(2,1)} %param.13) | copy-start | bytes 7077892
  7.2 74.3 %all-gather.7.cloned.1.call-start = ((), (), s32[]{:S(2)}) async-start(), calls=%async_computation.9 | async-start | bytes 4259840 | tf_op jit(solution)/shard_map/all_gather | solution.py:48
  12.7 137.7 %all-gather.5.cloned.1.call-start = ((), (), s32[]{:S(2)}) async-start(), calls=%async_computation.8 | async-start | bytes 4259840 | tf_op jit(solution)/shard_map/all_gather | solution.py:47
  14.8 828.0 %reduce-scatter.7.cloned.1.call-start = ((), (), s32[]{:S(2)}) async-start(), calls=%async_computation.5 | async-start | bytes 8519680 | tf_op jit(solution)/shard_map/reduce_scatter | solution.py:80
  159.1 9.1 copy-start.4
  178.1 8.8 slice-start
  180.5 6.3 slice-start.1
  186.8 7.4 copy-start.7
  203.0 9.1 copy-start.4
  212.1 5.5 copy-start.2
  221.9 11.4 slice-start
  224.4 9.0 slice-start.1
  233.3 7.4 copy-start.7
  249.5 9.1 copy-start.4
  258.6 5.5 copy-start.2
  268.4 11.4 slice-start
  270.8 9.0 slice-start.1
  279.8 7.4 copy-start.7
  296.0 9.1 copy-start.4
  305.1 5.5 copy-start.2
  314.9 11.4 slice-start
  317.3 9.0 slice-start.1
  326.3 7.4 copy-start.7
  342.5 9.1 copy-start.4
  351.6 5.5 copy-start.2
  361.4 11.4 slice-start
  363.8 9.0 slice-start.1
  372.8 7.4 copy-start.7
  389.0 9.1 copy-start.4
  398.1 5.5 copy-start.2
  407.9 11.4 slice-start
  410.3 9.0 slice-start.1
  419.3 7.4 copy-start.7
  435.4 9.1 copy-start.4
  444.6 5.5 copy-start.2
  454.4 11.4 slice-start
  456.8 9.0 slice-start.1
  465.7 7.4 copy-start.7
  481.9 9.1 copy-start.4
  491.0 5.5 copy-start.2
  500.8 11.4 slice-start
  503.3 9.0 slice-start.1
  512.2 7.4 copy-start.7
  519.6 688.4 %reduce-scatter.9.cloned.1.call-start = ((), (), s32[]{:S(2)}) async-start(), calls=%async_computation.6 | async-start | bytes 8519680 | tf_op jit(solution)/shard_map/reduce_scatter | solution.py:81
  520.2 322.5 %copy-start.8 = (bf16[1536,128]{1,0:T(8,128)(2,1)S(1)}, bf16[1536,128]{1,0:T(8,128)(2,1)}, u32[]{:S(2)}) copy-start(bf16[1536,128]{1,0:T(8,128)(2,1)} %param.11) | copy-start | bytes 1179652
  520.2 746.2 %reduce-scatter.5.cloned.1.call-start = ((), (), s32[]{:S(2)}) async-start(), calls=%async_computation.4 | async-start | bytes 2359296 | tf_op jit(solution)/shard_map/reduce_scatter | solution.py:79
  523.4 684.6 %copy-start.9 = (bf16[1536,128]{1,0:T(8,128)(2,1)S(1)}, bf16[1536,128]{1,0:T(8,128)(2,1)}, u32[]{:S(2)}) copy-start(bf16[1536,128]{1,0:T(8,128)(2,1)} %param.12) | copy-start | bytes 1179652
  523.5 758.0 %reduce-scatter.11.cloned.1.call-start = ((), (), s32[]{:S(2)}) async-start(), calls=%async_computation.7 | async-start | bytes 2359296 | tf_op jit(solution)/shard_map/reduce_scatter | solution.py:83
  (34 other events, 139.9 us)
Sparse Core Ops, SparseCore 0:
  12.8 68.6 all-gather.6
  84.4 65.9 all-gather.4
  519.8 322.9 reduce-scatter.6
  845.0 363.0 reduce-scatter.8
  1210.2 56.1 reduce-scatter.4
  1268.6 12.7 reduce-scatter.10
where the time goes:
time: 1290 us
  waiting for transfers between devices  873 us (68%)
  matrix products  245 us (19%)
  other arithmetic  98 us (8%)
  local copies, waits for them, and re-layouts  53.5 us (4%)
  between operations  14.2 us (1%)
    reduce_scatter x1, waiting for transfers between devices, local_step(): lax.psum_scatter(dv_part, 'cp', scatter_dimension=0, tiled=True)  362 us
    reduce_scatter x1, waiting for transfers between devices, local_step(): lax.psum_scatter(dk_part, 'cp', scatter_dimension=0, tiled=True)  315 us
    convert_element_type x8, other arithmetic, block_step(): prob_bf = jnp.exp(scores - log_norm).astype(jnp.bfloat16)  73 us
    dot_general x8, matrix products, block_step(): jnp.einsum('hgqk,qhgd->khd', d_score, q_blk, preferred_element_type=jnp.f...  69 us
    all_gather x1, waiting for transfers between devices, local_step(): keys_all = lax.all_gather(keys_loc, 'cp', axis=0, tiled=True)  68.9 us
    all_gather x1, waiting for transfers between devices, local_step(): values_all = lax.all_gather(values_loc, 'cp', axis=0, tiled=True)  57.4 us
    reduce_scatter x1, waiting for transfers between devices, local_step(): lax.psum_scatter(y_part, 'tp', scatter_dimension=0, tiled=True)  55.3 us
    while x144, local copies, waits for them, and re-layouts  44.2 us
  transfers between devices with their start and end apart: 6, of which 6 were waited for; matrix products, arithmetic and copies ran while one was open for 2% of the time, Pallas kernels for 0%

commit v1 on v0

v1 whole, which is shorter than its diff:
```python
import functools
import math

import jax
import jax.numpy as jnp
from jax import lax
from jax.experimental import pallas as pl
from jax.experimental.pallas import tpu as pltpu
from jax.sharding import PartitionSpec as P

HEAD_DIM = 128
PIECE = 128
SIDE = 4
LOG2E = math.log2(math.e)
LOWEST = float(jnp.finfo(jnp.float32).min)
MESH = pl.DeviceIdType.MESH
BF = jnp.bfloat16
F32 = jnp.float32

THIRDS = ((0, 176), (176, 160), (336, 176))
AG_HALF = (96, 80, 96)
RS_HALF = (88, 80, 88)
ORDERS = ((2, 1, 0), (1, 0, 2), (0, 2, 1))
STRIDE = (16, 4, 1)
MAX_ROWS = 176


def dot(a, b):
    return lax.dot_general(a, b, (((1,), (0,)), ((), ())), preferred_element_type=F32)


def dot_ta(a, b):
    return lax.dot_general(a, b, (((0,), (0,)), ((), ())), preferred_element_type=F32)


def kernel(groups, qt_ref, q_ref, dot_ref, do_ref, kv_loc, o_out, dq_out, dkv_out,
           kv, dkv, m_ref, l_ref, acc, dqt, delta, ra0, ra1, ra2, sa0, sa1, sa2,
           local_sem, ag_send, ag_recv, rs_send, rs_recv):
    rank = lax.axis_index('cp')
    me = (rank // 16, lax.rem(rank // 4, 4), lax.rem(rank, 4))
    lanes = groups * PIECE
    width = groups * PIECE

    def coord(dim, off):
        return lax.rem(me[dim] + (off + SIDE), SIDE)

    def device(dim, off):
        return {'cp': rank + STRIDE[dim] * (coord(dim, off) - me[dim])}

    def part(ref, phase, third, q, rows, gathered):
        order = ORDERS[third]
        idx = [None, None, None]
        for p, dim in enumerate(order):
            if p == phase:
                idx[dim] = q
            elif (p < phase) == gathered:
                idx[dim] = slice(None)
            else:
                idx[dim] = me[dim]
        return ref.at[idx[0], idx[1], idx[2], pl.ds(rows[0], rows[1])]

    barrier = pltpu.get_barrier_semaphore()
    for dim in range(3):
        for off in (1, -1):
            pl.semaphore_signal(barrier, inc=1, device_id=device(dim, off), device_id_type=MESH)
    own = pltpu.make_async_copy(kv_loc, kv.at[me[0], me[1], me[2]], local_sem)
    own.start()
    pl.semaphore_wait(barrier, 6)
    own.wait()

    sends = []

    def push(src, dst, send, recv, dim, off):
        copy = pltpu.make_async_remote_copy(src_ref=src, dst_ref=dst, send_sem=send, recv_sem=recv,
                                            device_id=device(dim, off), device_id_type=MESH)
        copy.start()
        sends.append(copy)

    def landed(ref, sem):
        pltpu.make_async_copy(ref, ref, sem).wait()

    def ag_copy(phase, third, kind, q, rows):
        dim = ORDERS[third][phase]
        ref = part(kv, phase, third, q, rows, True)
        push(ref, ref, ag_send.at[third, phase, kind], ag_recv.at[third, phase, kind], dim, 1 if kind % 2 == 0 else -1)

    for phase in range(3):
        for third in range(3):
            dim = ORDERS[third][phase]
            start, size = THIRDS[third]
            for kind in (0, 1):
                ag_copy(phase, third, kind, me[dim], (start, size))
        for third in range(3):
            dim = ORDERS[third][phase]
            start, size = THIRDS[third]
            half = AG_HALF[third]
            halves = ((start, half), (start + half, size - half))
            for kind in (0, 1):
                q = coord(dim, -1 if kind == 0 else 1)
                landed(part(kv, phase, third, q, (start, size), True), ag_recv.at[third, phase, kind])
                ag_copy(phase, third, 2 + kind, q, halves[kind])
        for third in range(3):
            dim = ORDERS[third][phase]
            start, size = THIRDS[third]
            half = AG_HALF[third]
            halves = ((start, half), (start + half, size - half))
            for kind in (0, 1):
                landed(part(kv, phase, third, coord(dim, 2), halves[kind], True), ag_recv.at[third, phase, 2 + kind])

    scale = HEAD_DIM ** -0.5
    c = scale * LOG2E

    def block(j):
        return j // 16, lax.rem(j // 4, 4), lax.rem(j, 4)

    def lane_mask(keys):
        krow = lax.broadcasted_iota(jnp.int32, (keys, width), 0)
        qrow = lax.rem(lax.broadcasted_iota(jnp.int32, (keys, width), 1), PIECE)
        return krow - (keys - PIECE) <= qrow

    def fwd_tile(j, keys, half, masked):
        jz, jy, jx = block(j)
        k = kv[jz, jy, jx, 0:keys, :]
        v = kv[jz, jy, jx, 256:256 + keys, :]
        ql = pl.ds(half * width, width)
        s = dot(k, qt_ref[:, ql])
        if masked:
            s = jnp.where(lane_mask(keys), s, LOWEST)
        m_old = m_ref[:, ql]
        m_new = jnp.maximum(m_old, jnp.max(s, axis=0, keepdims=True))
        alpha = jnp.exp2((m_old - m_new) * c)
        p = jnp.exp2((s - m_new) * c)
        m_ref[:, ql] = m_new
        l_ref[:, ql] = l_ref[:, ql] * alpha + jnp.sum(p, axis=0, keepdims=True)
        acc[:, ql] = acc[:, ql] * alpha + dot_ta(v, p.astype(BF))

    m_ref[...] = jnp.full(m_ref.shape, LOWEST, F32)
    l_ref[...] = jnp.zeros(l_ref.shape, F32)
    acc[...] = jnp.zeros(acc.shape, F32)
    fwd_tile(rank, 128, 0, True)
    fwd_tile(rank, 256, 1, True)

    def fwd_low(j, carry):
        fwd_tile(j, 128, 0, False)
        fwd_tile(j, 128, 1, False)
        return carry

    def fwd_high(j, carry):
        fwd_tile(j, 256, 1, False)
        return carry

    lax.fori_loop(0, rank, fwd_low, 0)
    lax.fori_loop(rank + 1, 64, fwd_high, 0)

    l = l_ref[...]
    o = (acc[...] * (1.0 / l)).astype(BF)
    o_out[...] = o
    delta[...] = jnp.sum(dot_ref[...].astype(F32) * o.astype(F32), axis=0, keepdims=True)
    m_ref[...] = m_ref[...] * c + jnp.log(l) * LOG2E
    dqt[...] = jnp.zeros(dqt.shape, F32)

    def bwd_tile(j, keys, half, masked):
        jz, jy, jx = block(j)
        k = kv[jz, jy, jx, 0:keys, :]
        v = kv[jz, jy, jx, 256:256 + keys, :]
        ql = pl.ds(half * width, width)
        s = dot(k, qt_ref[:, ql])
        p = jnp.exp2(s * c - m_ref[:, ql])
        if masked:
            p = jnp.where(lane_mask(keys), p, 0.0)
        pb = p.astype(BF)
        dp = dot(v, dot_ref[:, ql])
        ds = (pb.astype(F32) * (dp - delta[:, ql])).astype(BF)
        dqt[:, ql] += dot_ta(k, ds)
        return dot(ds, q_ref[ql, :]) * scale, dot(pb, do_ref[ql, :])

    zero = jnp.zeros((PIECE, HEAD_DIM), F32)

    def store(j, keys, dk, dv):
        jz, jy, jx = block(j)
        dkv[jz, jy, jx, 0:keys, :] = dk
        dkv[jz, jy, jx, 256:256 + keys, :] = dv
        if keys == 128:
            dkv[jz, jy, jx, 128:256, :] = zero
            dkv[jz, jy, jx, 384:512, :] = zero

    def bwd_low(j, carry):
        dk0, dv0 = bwd_tile(j, 128, 0, False)
        dk1, dv1 = bwd_tile(j, 128, 1, False)
        store(j, 128, dk0 + dk1, dv0 + dv1)
        return carry

    def bwd_high(j, carry):
        store(j, 256, *bwd_tile(j, 256, 1, False))
        return carry

    store(rank, 256, *bwd_tile(rank, 256, 1, True))
    dk0, dv0 = bwd_tile(rank, 128, 0, True)
    dkv[me[0], me[1], me[2], 0:128, :] += dk0
    dkv[me[0], me[1], me[2], 256:384, :] += dv0
    lax.fori_loop(0, rank, bwd_low, 0)
    lax.fori_loop(rank + 1, 64, bwd_high, 0)
    dq_out[...] = (dqt[...] * scale).astype(BF)

    ra = (ra0, ra1, ra2)
    sa = (sa0, sa1, sa2)

    def rs_split(third):
        start, size = THIRDS[third]
        half = RS_HALF[third]
        return (start, half), (start + half, size - half)

    def add_rows(phase, third, q, rows, sources):
        order = ORDERS[third]
        free = [order[p] for p in range(phase + 1, 3)]

        def one(u, carry):
            idx = {d: me[d] for d in order[:phase]}
            idx[order[phase]] = q
            sub = {}
            for n, d in enumerate(sorted(free)):
                sub[d] = lax.rem(u // SIDE ** (len(free) - 1 - n), SIDE)
            idx.update(sub)
            lead = tuple(sub[d] for d in sorted(free))
            total = dkv[idx[0], idx[1], idx[2], rows[0]:rows[0] + rows[1], :]
            for ref, offset in sources:
                total = total + ref[(*lead, slice(offset, offset + rows[1]), slice(None))]
            dkv[idx[0], idx[1], idx[2], rows[0]:rows[0] + rows[1], :] = total
            return carry

        lax.fori_loop(0, SIDE ** len(free), one, 0)

    for phase in range(3):
        lead = (slice(None),) * (2 - phase)

        def stage(third, sign, offset, size):
            return sa[phase].at[(third, sign, *lead, pl.ds(offset, size))]

        def relay(third, sign, size):
            return ra[phase].at[(third, sign, *lead, pl.ds(0, size))]

        def rs_push(third, kind, q, rows, dst):
            dim = ORDERS[third][phase]
            push(part(dkv, phase, third, q, rows, False), dst, rs_send.at[third, phase, kind],
                 rs_recv.at[third, phase, kind], dim, 1 if kind % 2 == 0 else -1)

        for third in range(3):
            dim = ORDERS[third][phase]
            h = rs_split(third)
            for sign in (0, 1):
                rs_push(third, sign, coord(dim, 2), h[sign], relay(third, sign, h[sign][1]))
        for third in range(3):
            dim = ORDERS[third][phase]
            h = rs_split(third)
            for sign in (0, 1):
                other = h[1 - sign]
                rs_push(third, 2 + sign, coord(dim, 1 if sign == 0 else -1), other,
                        stage(third, sign, other[0] - THIRDS[third][0], other[1]))
        for third in range(3):
            dim = ORDERS[third][phase]
            h = rs_split(third)
            for sign in (0, 1):
                q = coord(dim, 1 if sign == 0 else -1)
                landed(relay(third, sign, h[sign][1]), rs_recv.at[third, phase, sign])
                add_rows(phase, third, q, h[sign], [(ra[phase].at[third, sign], 0)])
                rs_push(third, 4 + sign, q, h[sign], stage(third, sign, h[sign][0] - THIRDS[third][0], h[sign][1]))
        for third in range(3):
            dim = ORDERS[third][phase]
            h = rs_split(third)
            for sign in (0, 1):
                other = h[1 - sign]
                landed(stage(third, sign, other[0] - THIRDS[third][0], other[1]), rs_recv.at[third, phase, 2 + sign])
                landed(stage(third, sign, h[sign][0] - THIRDS[third][0], h[sign][1]), rs_recv.at[third, phase, 4 + sign])
            add_rows(phase, third, me[dim], THIRDS[third], [(sa[phase].at[third, 0], 0), (sa[phase].at[third, 1], 0)])

    dkv_out[...] = dkv[me[0], me[1], me[2]].astype(BF)
    for copy in sends:
        copy.wait_send()


def attention(qt, q, dot_t, do, kv_loc, groups):
    lanes = 2 * groups * PIECE
    vmem = pl.BlockSpec(memory_space=pltpu.VMEM)
    return pl.pallas_call(
        functools.partial(kernel, groups),
        out_shape=(jax.ShapeDtypeStruct((HEAD_DIM, lanes), BF), jax.ShapeDtypeStruct((HEAD_DIM, lanes), BF),
                   jax.ShapeDtypeStruct((512, HEAD_DIM), BF)),
        in_specs=[vmem] * 5,
        out_specs=(vmem,) * 3,
        scratch_shapes=[
            pltpu.VMEM((4, 4, 4, 512, HEAD_DIM), BF),
            pltpu.VMEM((4, 4, 4, 512, HEAD_DIM), F32),
            pltpu.VMEM((1, lanes), F32), pltpu.VMEM((1, lanes), F32),
            pltpu.VMEM((HEAD_DIM, lanes), F32), pltpu.VMEM((HEAD_DIM, lanes), F32), pltpu.VMEM((1, lanes), F32),
            pltpu.VMEM((3, 2, 4, 4, 88, HEAD_DIM), F32), pltpu.VMEM((3, 2, 4, 88, HEAD_DIM), F32),
            pltpu.VMEM((3, 2, 88, HEAD_DIM), F32),
            pltpu.VMEM((3, 2, 4, 4, MAX_ROWS, HEAD_DIM), F32), pltpu.VMEM((3, 2, 4, MAX_ROWS, HEAD_DIM), F32),
            pltpu.VMEM((3, 2, MAX_ROWS, HEAD_DIM), F32),
            pltpu.SemaphoreType.DMA,
            pltpu.SemaphoreType.DMA((3, 3, 4)), pltpu.SemaphoreType.DMA((3, 3, 4)),
            pltpu.SemaphoreType.DMA((3, 3, 6)), pltpu.SemaphoreType.DMA((3, 3, 6)),
        ],
        compiler_params=pltpu.CompilerParams(collective_id=0, has_side_effects=True, vmem_limit_bytes=67043328),
        name='attention',
    )(qt, q, dot_t, do, kv_loc)


def dot_transposed(left, right):
    return lax.dot_general(left, right, (((1,), (1,)), ((), ())), preferred_element_type=F32)


def solution(mesh):
    row_spec = P(('dp', 'cp', 'tp'), None)

    def local_step(x_blk, dy_blk, w_query, w_key, w_value, w_out):
        groups = w_query.shape[1] // HEAD_DIM
        x_loc = lax.all_gather(x_blk, 'tp', axis=0, tiled=True)
        dy_loc = lax.all_gather(dy_blk, 'tp', axis=0, tiled=True)
        rows = x_loc.shape[0]

        def fold(a):
            return a.reshape(2, PIECE, groups, HEAD_DIM).transpose(0, 2, 1, 3).reshape(2 * groups * PIECE, HEAD_DIM)

        q = fold(jnp.dot(x_loc, w_query, preferred_element_type=F32).astype(BF))
        do = fold(dot_transposed(dy_loc, w_out).astype(BF))
        k = jnp.dot(x_loc, w_key, preferred_element_type=F32).astype(BF)
        v = jnp.dot(x_loc, w_value, preferred_element_type=F32).astype(BF)
        o_t, dq_t, dkv = attention(q.T, q, do.T, do, jnp.concatenate([k, v], axis=0), groups)

        def unfold(a):
            return a.reshape(HEAD_DIM, 2, groups, PIECE).transpose(1, 3, 2, 0).reshape(rows, groups * HEAD_DIM)

        y_part = jnp.dot(unfold(o_t), w_out, preferred_element_type=F32)
        y_blk = lax.psum_scatter(y_part, 'tp', scatter_dimension=0, tiled=True).astype(BF)
        dx_part = (dot_transposed(unfold(dq_t), w_query) + dot_transposed(dkv[:256], w_key)
                   + dot_transposed(dkv[256:], w_value))
        dx_blk = lax.psum_scatter(dx_part, 'tp', scatter_dimension=0, tiled=True).astype(BF)
        return y_blk, dx_blk

    return jax.shard_map(local_step, mesh=mesh,
                         in_specs=(row_spec, row_spec, P(None, 'tp'), P(None, 'tp'), P(None, 'tp'), P('tp', None)),
                         out_specs=(row_spec, row_spec), check_vma=False)
```

time: 1290 us -> 289 us (0.22)
  waiting for transfers between devices: 873 us -> 29.6 us
  matrix products: 245 us -> 10.9 us
  Pallas kernels: 0 us -> 215 us
  other arithmetic: 98 us -> 4.51 us
  local copies, waits for them, and re-layouts: 53.5 us -> 7.83 us
    reduce_scatter x4 -> x2, waiting for transfers between devices: 746 us -> 29.6 us  [the longest x1 16.3 us: local_step(): lax.psum_scatter(dx_part, 'tp', scatter_dimension=0, tiled=True).astype(BF)]
    dot_general x52 -> x4, matrix products: 233 us -> 5.66 us  [the longest x1 1.97 us: local_step(): v = jnp.dot(x_loc, w_value, preferred_element_type=F32).astype(BF)]
    pallas_call x0 -> x1, Pallas kernels: none -> 215 us  [attention(): pl.pallas_call(functools.partial(kernel, groups), out_shape=(jax.ShapeDty...]
    all_gather x2 -> x0, waiting for transfers between devices: 126 us -> none  [the longest x1 68.9 us: local_step(): keys_all = lax.all_gather(keys_loc, 'cp', axis=0, tiled=True)]
    convert_element_type x10 -> x2, other arithmetic: 76.8 us -> 3.84 us  [the longest x1 1.92 us: local_step(): lax.psum_scatter(y_part, 'tp', scatter_dimension=0, tiled=True).astype(BF)]
    while x146 -> x0, local copies, waits for them, and re-layouts: 45.6 us -> none
    reduce_sum x8 -> x0, other arithmetic: 18.2 us -> none  [block_step(): log_norm = jax.nn.logsumexp(scores, axis=-1, keepdims=True)]
  transfers between devices with their start and end apart: 6 -> 2, of which waited for: 6 -> 2; matrix products, arithmetic and copies ran while one was open for 2% -> 2% of each run, Pallas kernels for 0% -> 0%
where the time goes in v1:
time: 289 us; the launch traced here: 288 us
  Pallas kernels  215 us (74%)
  waiting for transfers between devices  29.6 us (10%)
  between operations  14.3 us (5%)
  matrix products  10.9 us (4%)
  local copies, waits for them, and re-layouts  7.83 us (3%)
  blocking collectives  5.85 us (2%)
  other arithmetic  4.51 us (2%)
    pallas_call x1, Pallas kernels, attention(): pl.pallas_call(functools.partial(kernel, groups), out_shape=(jax.ShapeDty...  215 us
    reduce_scatter x1, waiting for transfers between devices, local_step(): lax.psum_scatter(dx_part, 'tp', scatter_dimension=0, tiled=True).astype(BF)  16.3 us
    reduce_scatter x1, waiting for transfers between devices, local_step(): lax.psum_scatter(y_part, 'tp', scatter_dimension=0, tiled=True).astype(BF)  13.3 us
  transfers between devices with their start and end apart: 2, of which 2 were waited for; matrix products, arithmetic and copies ran while one was open for 2% of the time, Pallas kernels for 0%

profile of v1, /device:TPU:1, one launch (start us, length us, event | category | flops | bytes accessed | tf_op | source)
XLA Modules:
  0.0 288.3 jit_solution(4347246719839858041)
XLA Ops:
  7.2 0.0 copy-start.5
  7.2 0.0 copy-start.2
  7.2 0.0 reduce-scatter.5.cloned.1.call-start
  7.2 3.5 %all_gather.6 = bf16[256,1536]{1,0:T(8,128)(2,1)S(1)} all-gather(bf16[128,1536]{1,0:T(8,128)(2,1)} %param.6), channel_id=1, replica_groups=mesh['dp'=1,'tp'=2,'cp'=64] {'tp'}, dimensions={0}, use_global_device_ids=true | all-gather | bytes 1179648 | tf_op jit(solution)/shard_map/all_gather | solution.py:317
  10.7 2.0 convolution_convert_fusion.2
  12.7 0.0 copy-done.5
  12.7 1.0 convolution_convert_fusion.3
  13.7 0.8 convolution_convert_fusion.1
  14.5 0.0 copy-start.9
  14.5 0.0 copy-start.3
  14.5 0.2 copy.12
  14.7 0.1 reshape.28
  14.8 0.4 copy.13
  15.2 0.0 copy-start
  15.2 0.9 copy.16.qt_ref
  16.1 0.0 copy-done.9
  16.1 2.4 all_gather.7
  18.5 0.0 copy-done.3
  18.5 0.8 convolution_convert_fusion
  19.3 0.0 copy-done
  19.3 0.0 copy-start.10
  19.3 0.0 copy-start.11
  19.4 0.2 copy.14
  19.5 0.1 reshape.30
  19.6 0.4 copy.15
  20.1 0.8 copy-done.1
  20.8 0.9 copy.17.dot_ref
  21.8 0.7 pad_maximum_fusion.kv_loc
  22.4 215.3 %attention.1 = (bf16[128,1536]{1,0:T(8,128)(2,1)}, bf16[128,1536]{1,0:T(8,128)(2,1)}, bf16[512,128]{1,0:T(8,128)(2,1)}) custom-call(bf16[128,1536]{1,0:T(8,128)(2,1)} %copy.16.qt_ref, bf16[1536,128]{1,0:T(8,128)(2,1)} %bitcast.45, bf16[128,1536]{1,0:T(8,128)(2,1)} %copy.17.dot_ref, bf16[1536,128]{1,0:T(8,128)(2,1)} %bitcast.47, ...), custom_call_target="tpu_custom_call" | custom-call | tf_op jit(solution)/shard_map/attention/pallas_call | solution.py:284
  237.7 1.2 copy.20
  238.9 0.4 copy.21
  239.3 0.0 copy-start.6
  239.4 2.5 fusion
  241.9 0.0 copy-start.7
  242.0 0.4 convolution_add_fusion.1
  242.3 0.6 copy-done.7
  242.9 1.5 convolution_add_fusion
  244.5 0.0 reduce-scatter.5.cloned.1.call-update
  244.5 0.0 reduce-scatter.3.cloned.1.call-start
  244.5 0.2 copy.18
  244.8 0.4 copy.19
  245.2 0.9 copy-done.4
  246.1 1.9 fusion.3
  248.1 0.0 reduce-scatter.3.cloned.1.call-update
  248.1 16.3 %reduce-scatter.5.cloned.1.call-done = f32[128,1536]{1,0:T(8,128)} async-done(((f32[256,1536]{1,0:T(8,128)}), f32[128,1536]{1,0:T(8,128)}) %reduce-scatter.5.cloned.1.call-update) | async-done | bytes 786448 | tf_op jit(solution)/shard_map/reduce_scatter | solution.py:337
  264.4 1.9 convert_element_type.23
  266.3 13.3 %reduce-scatter.3.cloned.1.call-done = f32[128,1536]{1,0:T(8,128)} async-done(((f32[256,1536]{1,0:T(8,128)}), f32[128,1536]{1,0:T(8,128)}) %reduce-scatter.3.cloned.1.call-update) | async-done | bytes 786448 | tf_op jit(solution)/shard_map/reduce_scatter | solution.py:334
  279.6 1.9 convert_element_type.22
  (10 shorter events, 0.0 us)
Async XLA Ops:
  7.2 5.5 %copy-start.5 = (bf16[1536,128]{1,0:T(8,128)(2,1)S(1)}, bf16[1536,128]{1,0:T(8,128)(2,1)}, u32[]{:S(2)}) copy-start(bf16[1536,128]{1,0:T(8,128)(2,1)} %param.9) | copy-start | bytes 1179652
  7.2 6.5 %copy-start.2 = (bf16[1536,768]{1,0:T(8,128)(2,1)S(1)}, bf16[1536,768]{1,0:T(8,128)(2,1)}, u32[]{:S(2)}) copy-start(bf16[1536,768]{1,0:T(8,128)(2,1)} %param.8) | copy-start | bytes 7077892
  7.2 257.2 %reduce-scatter.5.cloned.1.call-start = ((), (), s32[]{:S(2)}) async-start(), calls=%async_computation.3 | async-start | bytes 2359296 | tf_op jit(solution)/shard_map/reduce_scatter | solution.py:337
  14.5 1.7 copy-start.9
  14.5 4.0 %copy-start.3 = (bf16[768,1536]{1,0:T(8,128)(2,1)S(1)}, bf16[768,1536]{1,0:T(8,128)(2,1)}, u32[]{:S(2)}) copy-start(bf16[768,1536]{1,0:T(8,128)(2,1)} %param.11) | copy-start | bytes 7077892
  15.2 4.1 %copy-start = (bf16[2,6,128,128]{3,2,1,0:T(8,128)(2,1)}, bf16[2,6,128,128]{3,2,1,0:T(8,128)(2,1)S(1)}, u32[]{:S(2)}) copy-start(bf16[2,6,128,128]{3,2,1,0:T(8,128)(2,1)S(1)} %copy.13) | copy-start | bytes 1179652
  19.3 2.4 copy-start.10
  19.3 2.4 copy-start.11
  20.1 0.8 copy-start.1
  239.3 2.6 copy-start.6
  239.4 2.6 copy-start.12
  241.9 1.0 copy-start.7
  242.9 1.6 copy-start.8
  244.5 1.7 copy-start.4
  244.5 35.1 %reduce-scatter.3.cloned.1.call-start = ((), (), s32[]{:S(2)}) async-start(), calls=%async_computation.2 | async-start | bytes 2359296 | tf_op jit(solution)/shard_map/reduce_scatter | solution.py:334
Sparse Core Ops, SparseCore 0:
  244.6 19.7 reduce-scatter.4
  266.7 12.8 reduce-scatter.2

commit v2 on v0

v2 whole, which is shorter than its diff:
```python
import functools
import math

import jax
import jax.numpy as jnp
from jax import lax
from jax.experimental import pallas as pl
from jax.experimental.pallas import tpu as pltpu
from jax.sharding import PartitionSpec as P

HEAD_DIM = 128
PIECE = 128
SIDE = 4
LOG2E = math.log2(math.e)
LOWEST = float(jnp.finfo(jnp.float32).min)
MESH = pl.DeviceIdType.MESH
BF = jnp.bfloat16
F32 = jnp.float32
ALL = slice(None)

AG_ROWS = ((0, 160), (160, 176), (336, 176))
AG_HALF = (80, 96, 96)
RS_ROWS = ((0, 168), (168, 176), (344, 168))
RS_HALF = (88, 88, 88)
STRIDE = (16, 4, 1)
PLANES = (0, 1, 3, 2)
AG_RINGS = ('0a', '1a', '2a', '2b', '2c') + tuple(f'{t}{p}{o}' for t in (0, 1) for p in 'bc' for o in range(4))
RS_RINGS = {'0z': (0, 0, 0), '1z': (1, 0, 0), '2z': (2, 0, 2), '2x': (2, 2, 1), '2y': (2, 1, 0)}
for off in range(4):
    RS_RINGS[f'0x{off}'] = (0, 2, 1)
    RS_RINGS[f'1y{off}'] = (1, 1, 1)
    RS_RINGS[f'0y{off}'] = (0, 1, 0)
    RS_RINGS[f'1x{off}'] = (1, 2, 0)
RS_NAMES = tuple(RS_RINGS)


def dot(a, b):
    return lax.dot_general(a, b, (((1,), (0,)), ((), ())), preferred_element_type=F32)


def dot_ta(a, b):
    return lax.dot_general(a, b, (((0,), (0,)), ((), ())), preferred_element_type=F32)


def dot_tb(a, b):
    return lax.dot_general(a, b, (((1,), (1,)), ((), ())), preferred_element_type=F32)


def rs_scratch():
    shapes = []
    for part, _, free in RS_RINGS.values():
        lead = (SIDE,) * free
        shapes.append(pltpu.VMEM((2, *lead, RS_HALF[part], HEAD_DIM), F32))
        shapes.append(pltpu.VMEM((2, *lead, RS_ROWS[part][1], HEAD_DIM), F32))
    return shapes


def kernel(groups, *refs):
    (qt_ref, q_ref, dot_ref, do_ref, kv_loc, wq_hbm, wk_hbm, wv_hbm, wo_hbm, y_out, dx_out,
     kv, dkv, m_ref, l_ref, acc, delta, kt, vt, wq, wk, wv, wo, rows_bf, y_part, y_recv, dx_part, dx_recv,
     local_sem, pair_send, pair_recv, ag_send, ag_recv, rs_send, rs_recv, *rs_bufs) = refs
    rank = lax.axis_index('cp')
    core = lax.axis_index('tp')
    me = (rank // 16, lax.rem(rank // 4, 4), lax.rem(rank, 4))
    width = groups * PIECE
    dqt = acc

    coords = [[lax.rem(me[dim] + off, SIDE) for off in range(SIDE)] for dim in range(3)]

    def coord(dim, off):
        return coords[dim][off % SIDE]

    def device(dim, off):
        return {'cp': rank + STRIDE[dim] * (coord(dim, off) - me[dim])}

    partner = {'tp': 1 - core}
    barrier = pltpu.get_barrier_semaphore()
    for dim in range(3):
        for off in (1, -1):
            pl.semaphore_signal(barrier, inc=1, device_id=device(dim, off), device_id_type=MESH)
    pl.semaphore_signal(barrier, inc=1, device_id=partner, device_id_type=MESH)
    own = pltpu.make_async_copy(kv_loc, kv.at[me[0], me[1], me[2]], local_sem.at[0])
    own.start()
    loads = [pltpu.make_async_copy(src, dst, local_sem.at[1 + n])
             for n, (src, dst) in enumerate(((wq_hbm, wq), (wk_hbm, wk), (wv_hbm, wv), (wo_hbm, wo)))]
    for load in loads:
        load.start()
    pl.semaphore_wait(barrier, 7)
    own.wait()

    sends = []

    def remote(src, dst, send, recv, to):
        return pltpu.make_async_remote_copy(src_ref=src, dst_ref=dst, send_sem=send, recv_sem=recv,
                                            device_id=to, device_id_type=MESH)

    def push(src, dst, send, recv, to):
        remote(src, dst, send, recv, to).start()

    def landed(ref, sem):
        pltpu.make_async_copy(ref, ref, sem).wait()

    def ag_where(name):
        third = int(name[0])
        z, y, x = me
        if third == 2:
            if name[1] == 'a':
                return third, 1, lambda q: (z, q, x)
            if name[1] == 'b':
                return third, 2, lambda q: (z, ALL, q)
            return third, 0, lambda q: (q, ALL, ALL)
        if name[1] == 'a':
            return third, 0, lambda q: (q, y, x)
        plane = coord(0, int(name[2]))
        if third == 0:
            if name[1] == 'b':
                return third, 1, lambda q: (plane, q, x)
            return third, 2, lambda q: (plane, ALL, q)
        if name[1] == 'b':
            return third, 2, lambda q: (plane, y, q)
        return third, 1, lambda q: (plane, q, ALL)

    def ag_ref(name, off, rows):
        third, dim, where = ag_where(name)
        return kv.at[(*where(coord(dim, off)), pl.ds(*rows))]

    def ag_split(third):
        start, size = AG_ROWS[third]
        return (start, AG_HALF[third]), (start + AG_HALF[third], size - AG_HALF[third])

    def ag_push(name, kind, off, rows):
        n = AG_RINGS.index(name)
        ref = ag_ref(name, off, rows)
        push(ref, ref, ag_send.at[n, kind], ag_recv.at[n, kind], device(ag_where(name)[1], 1 if kind % 2 == 0 else -1))
        sends.append(lambda: (ag_ref(name, off, rows), ag_send.at[n, kind]))

    def direct(*names):
        for name in names:
            for kind in (0, 1):
                ag_push(name, kind, 0, AG_ROWS[int(name[0])])

    def relay(*names):
        for name in names:
            third = int(name[0])
            for kind in (0, 1):
                off = -1 if kind == 0 else 1
                landed(ag_ref(name, off, AG_ROWS[third]), ag_recv.at[AG_RINGS.index(name), kind])
                ag_push(name, 2 + kind, off, ag_split(third)[kind])

    def done(*names):
        for name in names:
            for kind in (0, 1):
                landed(ag_ref(name, 2, ag_split(int(name[0]))[kind]), ag_recv.at[AG_RINGS.index(name), 2 + kind])

    def rs_where(name):
        z, y, x = me
        part = int(name[0])
        if name in ('0z', '1z'):
            return lambda q: (q, y, x)
        if name == '2z':
            return lambda q: (q, ALL, ALL)
        if name == '2x':
            return lambda q: (z, ALL, q)
        if name == '2y':
            return lambda q: (z, q, x)
        plane = coord(0, int(name[2]))
        return {'0x': lambda q: (plane, ALL, q), '1y': lambda q: (plane, q, ALL),
                '0y': lambda q: (plane, q, x), '1x': lambda q: (plane, y, q)}[name[:2]]

    def rs_split(part):
        start, size = RS_ROWS[part]
        return (start, RS_HALF[part]), (start + RS_HALF[part], size - RS_HALF[part])

    def rs_ref(name, q, rows):
        return dkv.at[(*rs_where(name)(q), pl.ds(*rows))]

    def rs_land(name, kind, sign):
        part, _, free = RS_RINGS[name]
        n = RS_NAMES.index(name)
        h = rs_split(part)
        lead = (ALL,) * free
        if kind == 0:
            return rs_bufs[2 * n].at[(sign, *lead, pl.ds(0, h[sign][1]))]
        rows = h[1 - sign] if kind == 1 else h[sign]
        return rs_bufs[2 * n + 1].at[(sign, *lead, pl.ds(rows[0] - RS_ROWS[part][0], rows[1]))]

    def rs_push(name, kind, sign, q, rows):
        n = RS_NAMES.index(name)
        push(rs_ref(name, q, rows), rs_land(name, kind, sign), rs_send.at[n, 2 * kind + sign],
             rs_recv.at[n, 2 * kind + sign], device(RS_RINGS[name][1], 1 if sign == 0 else -1))
        off = 2 if kind == 0 else 1 if sign == 0 else -1
        sends.append(lambda: (rs_ref(name, coord(RS_RINGS[name][1], off), rows), rs_send.at[n, 2 * kind + sign]))

    def rs_landed(name, kind, sign):
        landed(rs_land(name, kind, sign), rs_recv.at[RS_NAMES.index(name), 2 * kind + sign])

    def rs_add(name, q, rows, sources):
        free = RS_RINGS[name][2]
        where = rs_where(name)(q)

        def one(u, carry):
            sub = [lax.rem(u // SIDE ** (free - 1 - n), SIDE) for n in range(free)]
            left = iter(sub)
            idx = tuple(next(left) if w is ALL else w for w in where)
            total = dkv[(*idx, slice(rows[0], rows[0] + rows[1]), ALL)]
            for ref, offset in sources:
                total = total + ref[(*sub, slice(offset, offset + rows[1]), ALL)]
            dkv[(*idx, slice(rows[0], rows[0] + rows[1]), ALL)] = total
            return carry

        if free:
            lax.fori_loop(0, SIDE ** free, one, 0)
        else:
            one(0, 0)

    def rs_far(name, signs=(0, 1)):
        part, dim, _ = RS_RINGS[name]
        for sign in signs:
            rs_push(name, 0, sign, coord(dim, 2), rs_split(part)[sign])

    def rs_raw(name, signs=(0, 1)):
        part, dim, _ = RS_RINGS[name]
        for sign in signs:
            rs_push(name, 1, sign, coord(dim, 1 if sign == 0 else -1), rs_split(part)[1 - sign])

    def rs_mid(name, signs=(0, 1)):
        part, dim, _ = RS_RINGS[name]
        n = RS_NAMES.index(name)
        for sign in signs:
            rows = rs_split(part)[sign]
            q = coord(dim, 1 if sign == 0 else -1)
            rs_landed(name, 0, sign)
            rs_add(name, q, rows, [(rs_bufs[2 * n].at[sign], 0)])
            rs_push(name, 2, sign, q, rows)

    def rs_fin(name):
        part, dim, _ = RS_RINGS[name]
        n = RS_NAMES.index(name)
        for kind in (1, 2):
            for sign in (0, 1):
                rs_landed(name, kind, sign)
        rs_add(name, me[dim], RS_ROWS[part], [(rs_bufs[2 * n + 1].at[0], 0), (rs_bufs[2 * n + 1].at[1], 0)])

    def each(f, *names):
        for name in names:
            f(name)

    def rs_start(name):
        rs_far(name)
        rs_raw(name)

    scale = HEAD_DIM ** -0.5
    c = scale * LOG2E

    def lanes_of(half):
        return pl.ds(pl.multiple_of(half * width, PIECE), width)

    def allowed(j0, second, half):
        row = lax.broadcasted_iota(jnp.int32, (512, 1), 0)
        b = row // PIECE
        kpiece = j0 + b + second * (127 - 2 * (j0 + b))
        kpos = kpiece * PIECE + lax.rem(row, PIECE)
        qpiece = rank + half * (127 - 2 * rank)
        qpos = qpiece * PIECE + lax.rem(lax.broadcasted_iota(jnp.int32, (1, width), 1), PIECE)
        return kpos <= qpos

    def fwd_tile(half, mask):
        ql = lanes_of(half)
        s = dot(kt[...], qt_ref[:, ql])
        if mask is not None:
            s = jnp.where(mask, s, LOWEST)
        m_old = m_ref[:, ql]
        m_new = jnp.maximum(m_old, jnp.max(s, axis=0, keepdims=True))
        alpha = jnp.exp2((m_old - m_new) * c)
        p = jnp.exp2((s - m_new) * c)
        if mask is not None:
            p = jnp.where(mask, p, 0.0)
        m_ref[:, ql] = m_new
        l_ref[:, ql] = l_ref[:, ql] * alpha + jnp.sum(p, axis=0, keepdims=True)
        acc[:, ql] = acc[:, ql] * alpha + dot_ta(vt[...], p.astype(BF))

    def bwd_tile(half, mask):
        ql = lanes_of(half)
        k = kt[...]
        p = jnp.exp2(dot(k, qt_ref[:, ql]) * c - m_ref[:, ql])
        if mask is not None:
            p = jnp.where(mask, p, 0.0)
        pb = p.astype(BF)
        ds = (pb.astype(F32) * (dot(vt[...], dot_ref[:, ql]) - delta[:, ql])).astype(BF)
        dqt[:, ql] += dot_ta(k, ds)
        return dot(ds, q_ref[ql, :]) * scale, dot(pb, do_ref[ql, :])

    def group_loop(zp, yp, body):
        here = zp * 4 + yp
        mine = me[0] * 4 + me[1]
        mixed = here == mine
        high = here > mine
        count = jnp.where(mixed, 3, 2)

        def step(u, carry):
            second = jnp.logical_and(mixed, u == 2)
            half = jnp.where(jnp.logical_or(high, u == 2), 1, u)
            masked = jnp.logical_and(mixed, u != 1)

            @pl.when(high)
            def _():
                kt[...] = kv[zp, yp, pl.ds(2 * u, 2), 0:256, :].reshape(512, HEAD_DIM)
                vt[...] = kv[zp, yp, pl.ds(2 * u, 2), 256:512, :].reshape(512, HEAD_DIM)

            @pl.when(jnp.logical_and(jnp.logical_not(high), jnp.logical_not(second)))
            def _():
                kt[...] = kv[zp, yp, :, 0:128, :].reshape(512, HEAD_DIM)
                vt[...] = kv[zp, yp, :, 256:384, :].reshape(512, HEAD_DIM)

            @pl.when(second)
            def _():
                kt[...] = kv[zp, yp, :, 128:256, :].reshape(512, HEAD_DIM)
                vt[...] = kv[zp, yp, :, 384:512, :].reshape(512, HEAD_DIM)

            body(u, here * 4, second, high, half, masked)
            return carry

        lax.fori_loop(0, count, step, 0)

    def fwd_group(zp, yp):
        def body(u, j0, second, high, half, masked):
            @pl.when(jnp.logical_not(masked))
            def _():
                fwd_tile(half, None)

            @pl.when(masked)
            def _():
                fwd_tile(half, allowed(j0, jnp.where(second, 1, 0), half))

        group_loop(zp, yp, body)

    def bwd_group(zp, yp):
        dkv[zp, yp] = jnp.zeros((SIDE, 512, HEAD_DIM), F32)

        def body(u, j0, second, high, half, masked):
            def keep(dk, dv):
                @pl.when(high)
                def _():
                    dkv[zp, yp, pl.ds(2 * u, 2), 0:256, :] = dk.reshape(2, 256, HEAD_DIM)
                    dkv[zp, yp, pl.ds(2 * u, 2), 256:512, :] = dv.reshape(2, 256, HEAD_DIM)

                @pl.when(jnp.logical_not(high))
                def _():
                    dkv[zp, yp, :, 0:128, :] += dk.reshape(4, 128, HEAD_DIM)
                    dkv[zp, yp, :, 256:384, :] += dv.reshape(4, 128, HEAD_DIM)

            @pl.when(jnp.logical_not(masked))
            def _():
                keep(*bwd_tile(half, None))

            @pl.when(masked)
            def _():
                dk, dv = bwd_tile(half, allowed(j0, jnp.where(second, 1, 0), half))

                @pl.when(second)
                def _():
                    dkv[zp, yp, :, 128:256, :] = dk.reshape(4, 128, HEAD_DIM)
                    dkv[zp, yp, :, 384:512, :] = dv.reshape(4, 128, HEAD_DIM)

                @pl.when(jnp.logical_not(second))
                def _():
                    dkv[zp, yp, :, 0:128, :] += dk.reshape(4, 128, HEAD_DIM)
                    dkv[zp, yp, :, 256:384, :] += dv.reshape(4, 128, HEAD_DIM)

        group_loop(zp, yp, body)

    def run(compute, reverse, events):
        def step(g, carry):
            for at, ops in events.items():
                @pl.when(g == at)
                def _():
                    for f, *names in ops:
                        f(*names)
            d = g // 4
            if reverse:
                d = 3 - d
            off = d + d // 2 - 2 * (d // 3)
            compute(lax.rem(me[0] + off, SIDE), lax.rem(g, 4))
            return carry

        lax.fori_loop(0, 16, step, 0)

    m_ref[...] = jnp.full(m_ref.shape, LOWEST, F32)
    l_ref[...] = jnp.zeros(l_ref.shape, F32)
    acc[...] = jnp.zeros(acc.shape, F32)
    direct('0b0', '1b0', '2a', '0a', '1a')
    relay('0b0', '1b0', '2a', '0a', '1a')
    done('0b0')
    direct('0c0')
    done('1b0')
    direct('1c0')
    done('2a')
    direct('2b')
    direct('0b1', '1b1', '0b3', '1b3')
    relay('0c0', '1c0', '2b')
    relay('0b1', '1b1', '0b3', '1b3')
    done('2b')
    direct('2c')
    done('0b1')
    direct('0c1')
    done('1b1')
    direct('1c1')
    done('0b3', '1b3')
    direct('0c3', '1c3')
    done('0c0', '1c0')
    run(fwd_group, False, {
        1: [(done, '0a', '1a'), (direct, '0b2', '1b2'), (relay, '0c1', '1c1')],
        2: [(relay, '0b2', '1b2'), (relay, '0c3', '1c3')],
        3: [(done, '0b2', '1b2'), (direct, '0c2', '1c2')],
        4: [(done, '0c1', '1c1'), (relay, '2c')],
        6: [(relay, '0c2', '1c2')],
        8: [(done, '0c3', '1c3')],
        12: [(done, '0c2', '1c2', '2c')],
    })

    l = l_ref[...]
    o = (acc[...] * (1.0 / l)).astype(BF)
    delta[...] = jnp.sum(dot_ref[...].astype(F32) * o.astype(F32), axis=0, keepdims=True)
    m_ref[...] = m_ref[...] * c + jnp.log(l) * LOG2E

    def to_rows(value_t):
        for s in range(2):
            for h in range(groups):
                lo = (s * groups + h) * PIECE
                rows_bf[s, :, h * HEAD_DIM:(h + 1) * HEAD_DIM] = value_t[:, lo:lo + PIECE].T

    for load in loads:
        load.wait()
    to_rows(o)
    y_part[0] = dot(rows_bf[1 - core], wo[...])
    y_copy = remote(y_part.at[0], y_recv, pair_send.at[0], pair_recv.at[0], partner)
    y_copy.start()
    y_part[1] = dot(rows_bf[core], wo[...])

    dqt[...] = jnp.zeros(dqt.shape, F32)
    both = (0, 1)
    run(bwd_group, True, {
        4: [(rs_far, '0x2'), (rs_far, '1y2'), (rs_far, '2z'), (rs_raw, '0x2'), (rs_raw, '1y2')],
        6: [(rs_mid, '0x2'), (rs_mid, '1y2')],
        8: [(rs_start, '0x3'), (rs_start, '1y3'), (rs_raw, '2z', (1,)), (rs_mid, '2z', (1,)),
            (rs_fin, '0x2'), (rs_start, '0y2'), (rs_fin, '1y2'), (rs_start, '1x2')],
        10: [(rs_mid, '0x3'), (rs_mid, '1y3'), (rs_mid, '0y2'), (rs_mid, '1x2')],
        12: [(rs_start, '0x1'), (rs_start, '1y1'), (rs_raw, '2z', (0,)), (rs_mid, '2z', (0,)),
             (rs_fin, '0y2'), (rs_fin, '1x2'), (rs_far, '0z'), (rs_far, '1z'),
             (rs_fin, '0x3'), (rs_start, '0y3'), (rs_fin, '1y3'), (rs_start, '1x3')],
        14: [(rs_mid, '0x1'), (rs_mid, '1y1'), (rs_mid, '0y3'), (rs_mid, '1x3')],
    })
    each(rs_start, '0x0', '1y0')
    rs_fin('0x1')
    rs_start('0y1')
    rs_fin('1y1')
    rs_start('1x1')
    each(rs_fin, '0y3', '1x3')
    for name in ('0z', '1z'):
        rs_raw(name, (1,))
        rs_mid(name, (1,))
    y_copy.wait_recv()
    y_out[...] = (y_part[1] + y_recv[...]).astype(BF)
    to_rows((dqt[...] * scale).astype(BF))
    dx_part[0] = dot_tb(rows_bf[1 - core], wq[...])
    each(rs_mid, '0x0', '1y0', '0y1', '1x1')
    rs_fin('2z')
    rs_start('2x')
    dx_part[1] = dot_tb(rows_bf[core], wq[...])
    each(rs_fin, '0y1', '1x1')
    for name in ('0z', '1z'):
        rs_raw(name, (0,))
        rs_mid(name, (0,))
    rs_fin('0x0')
    rs_start('0y0')
    rs_fin('1y0')
    rs_start('1x0')
    rs_mid('2x')
    each(rs_mid, '0y0', '1x0')
    rs_fin('2x')
    rs_start('2y')
    each(rs_fin, '0y0', '1x0')
    rs_mid('2y')
    each(rs_fin, '0z', '1z', '2y')

    dk_own = dkv[me[0], me[1], me[2], 0:256, :].astype(BF)
    dv_own = dkv[me[0], me[1], me[2], 256:512, :].astype(BF)
    kt[0:256, :] = dk_own
    vt[0:256, :] = dv_own

    def add_kv(slot, side):
        rows = pl.ds(pl.multiple_of(side * PIECE, PIECE), PIECE)
        dx_part[slot] = dx_part[slot] + dot_tb(kt[rows, :], wk[...]) + dot_tb(vt[rows, :], wv[...])

    add_kv(0, 1 - core)
    dx_copy = remote(dx_part.at[0], dx_recv, pair_send.at[1], pair_recv.at[1], partner)
    dx_copy.start()
    add_kv(1, core)
    for sent in sends:
        landed(*sent())
    y_copy.wait_send()
    dx_copy.wait_recv()
    dx_out[...] = (dx_part[1] + dx_recv[...]).astype(BF)
    dx_copy.wait_send()


def attention(qt, q, dot_t, do, kv_loc, w_query, w_key, w_value, w_out, groups):
    lanes = 2 * groups * PIECE
    dim = w_query.shape[0]
    vmem = pl.BlockSpec(memory_space=pltpu.VMEM)
    anywhere = pl.BlockSpec(memory_space=pl.ANY)
    weights = (w_query, w_key, w_value, w_out)
    return pl.pallas_call(
        functools.partial(kernel, groups),
        out_shape=(jax.ShapeDtypeStruct((PIECE, dim), BF),) * 2,
        in_specs=[vmem] * 5 + [anywhere] * 4,
        out_specs=(vmem,) * 2,
        scratch_shapes=[
            pltpu.VMEM((4, 4, 4, 512, HEAD_DIM), BF),
            pltpu.VMEM((4, 4, 4, 512, HEAD_DIM), F32),
            pltpu.VMEM((1, lanes), F32), pltpu.VMEM((1, lanes), F32),
            pltpu.VMEM((HEAD_DIM, lanes), F32), pltpu.VMEM((1, lanes), F32),
            pltpu.VMEM((512, HEAD_DIM), BF), pltpu.VMEM((512, HEAD_DIM), BF),
            *[pltpu.VMEM(w.shape, BF) for w in weights],
            pltpu.VMEM((2, PIECE, groups * HEAD_DIM), BF),
            pltpu.VMEM((2, PIECE, dim), F32), pltpu.VMEM((PIECE, dim), F32),
            pltpu.VMEM((2, PIECE, dim), F32), pltpu.VMEM((PIECE, dim), F32),
            pltpu.SemaphoreType.DMA((5,)),
            pltpu.SemaphoreType.DMA((2,)), pltpu.SemaphoreType.DMA((2,)),
            pltpu.SemaphoreType.DMA((len(AG_RINGS), 4)), pltpu.SemaphoreType.DMA((len(AG_RINGS), 4)),
            pltpu.SemaphoreType.DMA((len(RS_NAMES), 6)), pltpu.SemaphoreType.DMA((len(RS_NAMES), 6)),
            *rs_scratch(),
        ],
        compiler_params=pltpu.CompilerParams(collective_id=0, has_side_effects=True, vmem_limit_bytes=67043328),
        name='attention',
    )(qt, q, dot_t, do, kv_loc, *weights)


def solution(mesh):
    row_spec = P(('dp', 'cp', 'tp'), None)

    def local_step(x_blk, dy_blk, w_query, w_key, w_value, w_out):
        groups = w_query.shape[1] // HEAD_DIM
        x_loc = lax.all_gather(x_blk, 'tp', axis=0, tiled=True)
        dy_loc = lax.all_gather(dy_blk, 'tp', axis=0, tiled=True)

        def fold(a):
            return a.reshape(2, PIECE, groups, HEAD_DIM).transpose(0, 2, 1, 3).reshape(2 * groups * PIECE, HEAD_DIM)

        q = fold(jnp.dot(x_loc, w_query, preferred_element_type=F32).astype(BF))
        do = fold(dot_tb(dy_loc, w_out).astype(BF))
        k = jnp.dot(x_loc, w_key, preferred_element_type=F32).astype(BF)
        v = jnp.dot(x_loc, w_value, preferred_element_type=F32).astype(BF)
        return attention(q.T, q, do.T, do, jnp.concatenate([k, v], axis=0), w_query, w_key, w_value, w_out, groups)

    return jax.shard_map(local_step, mesh=mesh,
                         in_specs=(row_spec, row_spec, P(None, 'tp'), P(None, 'tp'), P(None, 'tp'), P('tp', None)),
                         out_specs=(row_spec, row_spec), check_vma=False)
```

time: 1290 us -> 188 us (0.15)
  waiting for transfers between devices: 873 us -> 0 us
  matrix products: 245 us -> 4.57 us
  Pallas kernels: 0 us -> 167 us
  other arithmetic: 98 us -> 1.76 us
  local copies, waits for them, and re-layouts: 53.5 us -> 7.57 us
  between operations: 14.2 us -> 0.75 us
    reduce_scatter x4 -> x0, waiting for transfers between devices: 746 us -> none  [the longest x1 362 us: local_step(): lax.psum_scatter(dv_part, 'cp', scatter_dimension=0, tiled=True)]
    dot_general x56 -> x4, matrix products: 245 us -> 4.57 us  [the longest x1 1.98 us: local_step(): v = jnp.dot(x_loc, w_value, preferred_element_type=F32).astype(BF)]
    pallas_call x0 -> x1, Pallas kernels: none -> 167 us  [attention(): pl.pallas_call(functools.partial(kernel, groups), out_shape=(jax.ShapeDty...]
    all_gather x2 -> x0, waiting for transfers between devices: 126 us -> none  [the longest x1 68.9 us: local_step(): keys_all = lax.all_gather(keys_loc, 'cp', axis=0, tiled=True)]
    convert_element_type x10 -> x0, other arithmetic: 76.8 us -> none  [the longest x8 73 us: block_step(): prob_bf = jnp.exp(scores - log_norm).astype(jnp.bfloat16)]
    while x146 -> x0, local copies, waits for them, and re-layouts: 45.6 us -> none
    reduce_sum x8 -> x0, other arithmetic: 18.2 us -> none  [block_step(): log_norm = jax.nn.logsumexp(scores, axis=-1, keepdims=True)]
  transfers between devices with their start and end apart: 6 -> 0, of which waited for: 6 -> 0; matrix products, arithmetic and copies ran while one was open for 2% -> 0% of each run, Pallas kernels for 0% -> 0%
where the time goes in v2:
time: 188 us; the launch traced here: 187 us
  Pallas kernels  167 us (89%)
  local copies, waits for them, and re-layouts  7.57 us (4%)
  blocking collectives  5.85 us (3%)
  matrix products  4.57 us (2%)
    pallas_call x1, Pallas kernels, attention(): pl.pallas_call(functools.partial(kernel, groups), out_shape=(jax.ShapeDty...  167 us
    unnamed x14, local copies, waits for them, and re-layouts  4.32 us

profile of v2, /device:TPU:1, one launch (start us, length us, event | category | flops | bytes accessed | tf_op | source)
XLA Modules:
  0.0 187.3 jit_solution(6500800069489217938)
XLA Ops:
  0.6 0.0 copy-start.4
  0.6 0.0 copy-start.2
  0.7 3.5 %all_gather.6 = bf16[256,1536]{1,0:T(8,128)(2,1)S(1)} all-gather(bf16[128,1536]{1,0:T(8,128)(2,1)} %param.6), channel_id=1, replica_groups=mesh['dp'=1,'tp'=2,'cp'=64] {'tp'}, dimensions={0}, use_global_device_ids=true | all-gather | bytes 1179648 | tf_op jit(solution)/shard_map/all_gather | solution.py:544
  4.1 2.0 %convolution_convert_fusion.2 = bf16[256,128]{1,0:T(8,128)(2,1)} fusion(bf16[256,1536]{1,0:T(8,128)(2,1)S(1)} %all_gather.6, bf16[1536,128]{1,0:T(8,128)(2,1)} %refs_7_.1), kind=kOutput, calls=%fused_computation.2 | convolution fusion | flops 100696064 | bytes 1245184 | tf_op jit(solution)/shard_map/dot_general | solution.py:553
  6.1 0.0 copy-done.4
  6.1 1.0 convolution_convert_fusion.3
  7.1 0.0 copy-done.2
  7.1 0.8 convolution_convert_fusion.1
  7.9 0.0 copy-start.5
  7.9 0.0 copy-start.3
  7.9 0.2 copy.12
  8.1 0.1 reshape.16
  8.2 0.4 copy.13
  8.6 0.0 copy-start
  8.7 1.8 pad_maximum_fusion.refs_4_
  10.4 0.9 copy.16.refs_0_
  11.3 0.0 copy-done.5
  11.3 2.4 %all_gather.7 = bf16[256,1536]{1,0:T(8,128)(2,1)S(1)} all-gather(bf16[128,1536]{1,0:T(8,128)(2,1)S(1)} %copy-done.5), channel_id=1, replica_groups=mesh['dp'=1,'tp'=2,'cp'=64] {'tp'}, dimensions={0}, use_global_device_ids=true | all-gather | bytes 1179648 | tf_op jit(solution)/shard_map/all_gather | solution.py:545
  13.7 0.0 copy-done.3
  13.7 0.8 convolution_convert_fusion
  14.5 0.0 copy-done
  14.5 0.2 copy.14
  14.7 0.1 reshape.18
  14.8 0.4 copy.15
  15.3 0.0 copy-start.1
  15.3 0.8 copy-done.1
  16.0 0.9 copy.17.refs_2_
  17.0 166.8 %attention.1 = (bf16[128,1536]{1,0:T(8,128)(2,1)}, bf16[128,1536]{1,0:T(8,128)(2,1)}) custom-call(bf16[128,1536]{1,0:T(8,128)(2,1)} %copy.16.refs_0_, bf16[1536,128]{1,0:T(8,128)(2,1)} %bitcast.21, bf16[128,1536]{1,0:T(8,128)(2,1)} %copy.17.refs_2_, bf16[1536,128]{1,0:T(8,128)(2,1)} %bitcast.23, bf16[512,128]{1,0:T(8,128)(2,1)} %pad_maximum_fusion.refs_4_, ...), custom_call_target="tpu_custom_call" | custom-call | tf_op jit(solution)/shard_map/attention/pallas_call | solution.py:513
  183.7 1.8 copy.20
  185.5 1.8 copy.21
Async XLA Ops:
  0.6 5.5 %copy-start.4 = (bf16[1536,128]{1,0:T(8,128)(2,1)S(1)}, bf16[1536,128]{1,0:T(8,128)(2,1)}, u32[]{:S(2)}) copy-start(bf16[1536,128]{1,0:T(8,128)(2,1)} %refs_6_.1) | copy-start | bytes 1179652
  0.6 6.5 %copy-start.2 = (bf16[1536,768]{1,0:T(8,128)(2,1)S(1)}, bf16[1536,768]{1,0:T(8,128)(2,1)}, u32[]{:S(2)}) copy-start(bf16[1536,768]{1,0:T(8,128)(2,1)} %refs_5_.1) | copy-start | bytes 7077892
  7.9 3.4 %copy-start.5 = (bf16[128,1536]{1,0:T(8,128)(2,1)S(1)}, bf16[128,1536]{1,0:T(8,128)(2,1)}, u32[]{:S(2)}) copy-start(bf16[128,1536]{1,0:T(8,128)(2,1)} %param.7) | copy-start | bytes 1179652
  7.9 5.8 %copy-start.3 = (bf16[768,1536]{1,0:T(8,128)(2,1)S(1)}, bf16[768,1536]{1,0:T(8,128)(2,1)}, u32[]{:S(2)}) copy-start(bf16[768,1536]{1,0:T(8,128)(2,1)} %refs_8_.1) | copy-start | bytes 7077892
  8.6 5.9 %copy-start = (bf16[2,6,128,128]{3,2,1,0:T(8,128)(2,1)}, bf16[2,6,128,128]{3,2,1,0:T(8,128)(2,1)S(1)}, u32[]{:S(2)}) copy-start(bf16[2,6,128,128]{3,2,1,0:T(8,128)(2,1)S(1)} %copy.13) | copy-start | bytes 1179652
  15.3 0.8 copy-start.1

commit v3 on v2

--- a/solution.py
+++ b/solution.py
@@ -1,3 +1,4 @@
+import collections
 import functools
 import math
 
@@ -18,19 +19,21 @@
 F32 = jnp.float32
 ALL = slice(None)
 
-AG_ROWS = ((0, 160), (160, 176), (336, 176))
-AG_HALF = (80, 96, 96)
-RS_ROWS = ((0, 168), (168, 176), (344, 168))
-RS_HALF = (88, 88, 88)
+AG_ROWS = ((0, 160), (160, 192), (352, 160))
+AG_HALF = (80, 96, 80)
+RS_ROWS = ((0, 160), (160, 160), (320, 192), (320, 96), (416, 96))
+RS_HALF = (80, 80, 96, 48, 48)
 STRIDE = (16, 4, 1)
-PLANES = (0, 1, 3, 2)
-AG_RINGS = ('0a', '1a', '2a', '2b', '2c') + tuple(f'{t}{p}{o}' for t in (0, 1) for p in 'bc' for o in range(4))
-RS_RINGS = {'0z': (0, 0, 0), '1z': (1, 0, 0), '2z': (2, 0, 2), '2x': (2, 2, 1), '2y': (2, 1, 0)}
+AG_RINGS = ('0a', '1a', '2a', '1c0') + tuple(n + str(o) for n in ('0b', '1b', '0r', '2b', '2c') for o in range(4)) + tuple(
+    n + str(o) for n in ('0c', '1c') for o in range(1, 4))
+RS_RINGS = {'0z': (0, 0, 0), '1z': (1, 0, 0), '3x': (3, 2, 1), '3y': (3, 1, 0), '4y': (4, 1, 1), '4x': (4, 2, 0)}
 for off in range(4):
-    RS_RINGS[f'0x{off}'] = (0, 2, 1)
+    RS_RINGS[f'2z{off}'] = (2, 0, 1)
     RS_RINGS[f'1y{off}'] = (1, 1, 1)
     RS_RINGS[f'0y{off}'] = (0, 1, 0)
     RS_RINGS[f'1x{off}'] = (1, 2, 0)
+    for row in range(4):
+        RS_RINGS[f'0x{off}{row}'] = (0, 2, 0)
 RS_NAMES = tuple(RS_RINGS)
 
 
@@ -56,7 +59,7 @@
 
 
 def kernel(groups, *refs):
-    (qt_ref, q_ref, dot_ref, do_ref, kv_loc, wq_hbm, wk_hbm, wv_hbm, wo_hbm, y_out, dx_out,
+    (x_hbm, dy_hbm, wq_hbm, wk_hbm, wv_hbm, wo_hbm, y_out, dx_out, xs, dys, qt_ref, q_ref, dot_ref, do_ref,
      kv, dkv, m_ref, l_ref, acc, delta, kt, vt, wq, wk, wv, wo, rows_bf, y_part, y_recv, dx_part, dx_recv,
      local_sem, pair_send, pair_recv, ag_send, ag_recv, rs_send, rs_recv, *rs_bufs) = refs
     rank = lax.axis_index('cp')
@@ -79,14 +82,12 @@
         for off in (1, -1):
             pl.semaphore_signal(barrier, inc=1, device_id=device(dim, off), device_id_type=MESH)
     pl.semaphore_signal(barrier, inc=1, device_id=partner, device_id_type=MESH)
-    own = pltpu.make_async_copy(kv_loc, kv.at[me[0], me[1], me[2]], local_sem.at[0])
-    own.start()
-    loads = [pltpu.make_async_copy(src, dst, local_sem.at[1 + n])
-             for n, (src, dst) in enumerate(((wq_hbm, wq), (wk_hbm, wk), (wv_hbm, wv), (wo_hbm, wo)))]
-    for load in loads:
+    loads = {name: pltpu.make_async_copy(src, dst, local_sem.at[n]) for n, (name, src, dst) in enumerate((
+        ('x', x_hbm, xs.at[core]), ('wk', wk_hbm, wk), ('wv', wv_hbm, wv), ('dy', dy_hbm, dys.at[core]),
+        ('wq', wq_hbm, wq), ('wo', wo_hbm, wo)))}
+    for load in loads.values():
         load.start()
     pl.semaphore_wait(barrier, 7)
-    own.wait()
 
     sends = []
 
@@ -103,15 +104,16 @@
     def ag_where(name):
         third = int(name[0])
         z, y, x = me
+        if name[1] == 'a':
+            return (third, 1, lambda q: (z, q, x)) if third == 2 else (third, 0, lambda q: (q, y, x))
+        off = int(name[2])
+        if name[1] == 'r' or name[:2] == '2b':
+            row = coord(1, off)
+            return third, 2, lambda q: (z, row, q)
         if third == 2:
-            if name[1] == 'a':
-                return third, 1, lambda q: (z, q, x)
-            if name[1] == 'b':
-                return third, 2, lambda q: (z, ALL, q)
-            return third, 0, lambda q: (q, ALL, ALL)
-        if name[1] == 'a':
-            return third, 0, lambda q: (q, y, x)
-        plane = coord(0, int(name[2]))
+            column = coord(2, off)
+            return third, 0, lambda q: (q, ALL, column)
+        plane = coord(0, off)
         if third == 0:
             if name[1] == 'b':
                 return third, 1, lambda q: (plane, q, x)
@@ -154,18 +156,24 @@
 
     def rs_where(name):
         z, y, x = me
-        part = int(name[0])
         if name in ('0z', '1z'):
             return lambda q: (q, y, x)
-        if name == '2z':
-            return lambda q: (q, ALL, ALL)
-        if name == '2x':
+        if name == '3x':
             return lambda q: (z, ALL, q)
-        if name == '2y':
+        if name == '3y':
             return lambda q: (z, q, x)
+        if name == '4y':
+            return lambda q: (z, q, ALL)
+        if name == '4x':
+            return lambda q: (z, y, q)
+        if name[:2] == '2z':
+            row = coord(1, int(name[2]))
+            return lambda q: (q, row, ALL)
         plane = coord(0, int(name[2]))
-        return {'0x': lambda q: (plane, ALL, q), '1y': lambda q: (plane, q, ALL),
-                '0y': lambda q: (plane, q, x), '1x': lambda q: (plane, y, q)}[name[:2]]
+        if name[:2] == '0x':
+            row = coord(1, int(name[3]))
+            return lambda q: (plane, row, q)
+        return {'1y': lambda q: (plane, q, ALL), '0y': lambda q: (plane, q, x), '1x': lambda q: (plane, y, q)}[name[:2]]
 
     def rs_split(part):
         start, size = RS_ROWS[part]
@@ -264,11 +272,11 @@
         qpos = qpiece * PIECE + lax.rem(lax.broadcasted_iota(jnp.int32, (1, width), 1), PIECE)
         return kpos <= qpos
 
-    def fwd_tile(half, mask):
-        ql = lanes_of(half)
-        s = dot(kt[...], qt_ref[:, ql])
-        if mask is not None:
-            s = jnp.where(mask, s, LOWEST)
+    def scores(k, ql, mask=None):
+        s = dot(k, qt_ref[:, ql])
+        return s if mask is None else jnp.where(mask, s, LOWEST)
+
+    def online(s, v, ql, mask=None):
         m_old = m_ref[:, ql]
         m_new = jnp.maximum(m_old, jnp.max(s, axis=0, keepdims=True))
         alpha = jnp.exp2((m_old - m_new) * c)
@@ -277,7 +285,7 @@
             p = jnp.where(mask, p, 0.0)
         m_ref[:, ql] = m_new
         l_ref[:, ql] = l_ref[:, ql] * alpha + jnp.sum(p, axis=0, keepdims=True)
-        acc[:, ql] = acc[:, ql] * alpha + dot_ta(vt[...], p.astype(BF))
+        acc[:, ql] = acc[:, ql] * alpha + dot_ta(v, p.astype(BF))
 
     def bwd_tile(half, mask):
         ql = lanes_of(half)
@@ -323,19 +331,41 @@
         lax.fori_loop(0, count, step, 0)
 
     def fwd_group(zp, yp):
+        here = zp * 4 + yp
+        mine = me[0] * 4 + me[1]
+        first, last = slice(0, width), slice(width, 2 * width)
+
+        @pl.when(here < mine)
+        def _():
+            k = kv[zp, yp, :, 0:128, :].reshape(512, HEAD_DIM)
+            v = kv[zp, yp, :, 256:384, :].reshape(512, HEAD_DIM)
+            s0, s1 = scores(k, first), scores(k, last)
+            online(s0, v, first)
+            online(s1, v, last)
+
+        @pl.when(here > mine)
+        def _():
+            pairs = (slice(0, 2), slice(2, 4))
+            s0, s1 = (scores(kv[zp, yp, pair, 0:256, :].reshape(512, HEAD_DIM), last) for pair in pairs)
+            for s, pair in zip((s0, s1), pairs):
+                online(s, kv[zp, yp, pair, 256:512, :].reshape(512, HEAD_DIM), last)
+
         def body(u, j0, second, high, half, masked):
-            @pl.when(jnp.logical_not(masked))
-            def _():
-                fwd_tile(half, None)
-
-            @pl.when(masked)
-            def _():
-                fwd_tile(half, allowed(j0, jnp.where(second, 1, 0), half))
-
-        group_loop(zp, yp, body)
+            ql = lanes_of(half)
+            mask = allowed(j0, jnp.where(second, 1, 0), half)
+            online(scores(kt[...], ql, mask), vt[...], ql, mask)
+
+        @pl.when(here == mine)
+        def _():
+            group_loop(zp, yp, body)
 
     def bwd_group(zp, yp):
-        dkv[zp, yp] = jnp.zeros((SIDE, 512, HEAD_DIM), F32)
+        def first(dk, dv):
+            none = jnp.zeros((SIDE, 128, HEAD_DIM), F32)
+            dkv[zp, yp, :, 0:128, :] = dk.reshape(4, 128, HEAD_DIM)
+            dkv[zp, yp, :, 128:256, :] = none
+            dkv[zp, yp, :, 256:384, :] = dv.reshape(4, 128, HEAD_DIM)
+            dkv[zp, yp, :, 384:512, :] = none
 
         def body(u, j0, second, high, half, masked):
             def keep(dk, dv):
@@ -344,7 +374,11 @@
                     dkv[zp, yp, pl.ds(2 * u, 2), 0:256, :] = dk.reshape(2, 256, HEAD_DIM)
                     dkv[zp, yp, pl.ds(2 * u, 2), 256:512, :] = dv.reshape(2, 256, HEAD_DIM)
 
-                @pl.when(jnp.logical_not(high))
+                @pl.when(jnp.logical_and(jnp.logical_not(high), u == 0))
+                def _():
+                    first(dk, dv)
+
+                @pl.when(jnp.logical_and(jnp.logical_not(high), u != 0))
                 def _():
                     dkv[zp, yp, :, 0:128, :] += dk.reshape(4, 128, HEAD_DIM)
                     dkv[zp, yp, :, 256:384, :] += dv.reshape(4, 128, HEAD_DIM)
@@ -364,23 +398,24 @@
 
                 @pl.when(jnp.logical_not(second))
                 def _():
-                    dkv[zp, yp, :, 0:128, :] += dk.reshape(4, 128, HEAD_DIM)
-                    dkv[zp, yp, :, 256:384, :] += dv.reshape(4, 128, HEAD_DIM)
+                    first(dk, dv)
 
         group_loop(zp, yp, body)
+
+    def spiral(n):
+        return n + n // 2 - 2 * (n // 3)
 
     def run(compute, reverse, events):
         def step(g, carry):
             for at, ops in events.items():
                 @pl.when(g == at)
                 def _():
-                    for f, *names in ops:
-                        f(*names)
-            d = g // 4
+                    for f, *args in ops:
+                        f(*args)
+            d, r = g // 4, lax.rem(g, 4)
             if reverse:
-                d = 3 - d
-            off = d + d // 2 - 2 * (d // 3)
-            compute(lax.rem(me[0] + off, SIDE), lax.rem(g, 4))
+                d, r = 3 - d, 3 - r
+            compute(lax.rem(me[0] + spiral(d), SIDE), lax.rem(me[1] + spiral(r), SIDE))
             return carry
 
         lax.fori_loop(0, 16, step, 0)
@@ -388,35 +423,68 @@
     m_ref[...] = jnp.full(m_ref.shape, LOWEST, F32)
     l_ref[...] = jnp.zeros(l_ref.shape, F32)
     acc[...] = jnp.zeros(acc.shape, F32)
-    direct('0b0', '1b0', '2a', '0a', '1a')
-    relay('0b0', '1b0', '2a', '0a', '1a')
-    done('0b0')
-    direct('0c0')
+    loads['x'].wait()
+    x_copy = remote(xs.at[core], xs.at[core], pair_send.at[2], pair_recv.at[2], partner)
+    x_copy.start()
+    loads['wk'].wait()
+    loads['wv'].wait()
+
+    def project_kv(slot):
+        rows = xs[slot]
+        lo = pl.multiple_of(slot * PIECE, PIECE)
+        kv[me[0], me[1], me[2], pl.ds(lo, PIECE), :] = dot(rows, wk[...]).astype(BF)
+        kv[me[0], me[1], me[2], pl.ds(256 + lo, PIECE), :] = dot(rows, wv[...]).astype(BF)
+
+    def spread(rows, slot, flat, flat_t):
+        for h in range(groups):
+            block = rows[:, h * HEAD_DIM:(h + 1) * HEAD_DIM]
+            lo = pl.multiple_of((slot * groups + h) * PIECE, PIECE)
+            flat[pl.ds(lo, PIECE), :] = block
+            flat_t[:, pl.ds(lo, PIECE)] = block.T
+
+    def project_q(slot):
+        spread(dot(xs[slot], wq[...]).astype(BF), slot, q_ref, qt_ref)
+
+    def project_do(slot):
+        spread(dot_tb(dys[slot], wo[...]).astype(BF), slot, do_ref, dot_ref)
+
+    project_kv(core)
+    landed(xs.at[1 - core], pair_recv.at[2])
+    project_kv(1 - core)
+    direct('0r0', '1b0', '2b0', '0b0', '2a', '0a', '1a')
+    loads['dy'].wait()
+    dy_copy = remote(dys.at[core], dys.at[core], pair_send.at[3], pair_recv.at[3], partner)
+    dy_copy.start()
+    loads['wq'].wait()
+    project_q(core)
+    relay('1b0', '0r0', '0b0', '2a', '2b0')
+    direct('0r1', '0r3', '2b1', '2b3')
+    project_q(1 - core)
     done('1b0')
     direct('1c0')
+    relay('0a', '1a')
+    direct('0b1', '1b1', '0b3', '1b3')
+    done('0b0')
+    direct('0r2')
     done('2a')
-    direct('2b')
-    direct('0b1', '1b1', '0b3', '1b3')
-    relay('0c0', '1c0', '2b')
-    relay('0b1', '1b1', '0b3', '1b3')
-    done('2b')
-    direct('2c')
-    done('0b1')
-    direct('0c1')
-    done('1b1')
-    direct('1c1')
-    done('0b3', '1b3')
-    direct('0c3', '1c3')
-    done('0c0', '1c0')
+    direct('2b2', '2c0')
+    done('0r0', '2b0')
     run(fwd_group, False, {
-        1: [(done, '0a', '1a'), (direct, '0b2', '1b2'), (relay, '0c1', '1c1')],
-        2: [(relay, '0b2', '1b2'), (relay, '0c3', '1c3')],
-        3: [(done, '0b2', '1b2'), (direct, '0c2', '1c2')],
-        4: [(done, '0c1', '1c1'), (relay, '2c')],
-        6: [(relay, '0c2', '1c2')],
+        1: [(relay, '0r1', '2b1', '0r3', '2b3', '1c0'), (loads['wo'].wait,), (project_do, core),
+            (relay, '0b1', '1b1', '0b3', '1b3'), (done, '0r1', '2b1')],
+        2: [(relay, '0r2', '2b2'), (direct, '2c1', '2c3'), (done, '0b1'), (direct, '0c1'), (done, '1b1'), (direct, '1c1'),
+            (done, '0b3'), (direct, '0c3'), (done, '1b3'), (direct, '1c3'), (done, '0r3', '2b3')],
+        3: [(relay, '2c0'), (done, '0a', '1a'), (direct, '0b2', '1b2'), (done, '0r2', '2b2', '1c0'), (direct, '2c2'),
+            (landed, dys.at[1 - core], pair_recv.at[3]), (project_do, 1 - core), (relay, '0c1', '1c1')],
+        4: [(relay, '2c1', '2c3', '2c2'), (done, '0c1', '1c1')],
+        5: [(relay, '0c3', '1c3'), (relay, '0b2', '1b2')],
+        7: [(done, '0b2', '1b2'), (direct, '0c2', '1c2')],
         8: [(done, '0c3', '1c3')],
-        12: [(done, '0c2', '1c2', '2c')],
+        10: [(relay, '0c2', '1c2')],
+        12: [(done, '0c2', '1c2', '2c0', '2c1', '2c2', '2c3')],
     })
+    x_copy.wait_send()
+    dy_copy.wait_send()
 
     l = l_ref[...]
     o = (acc[...] * (1.0 / l)).astype(BF)
@@ -429,8 +497,6 @@
                 lo = (s * groups + h) * PIECE
                 rows_bf[s, :, h * HEAD_DIM:(h + 1) * HEAD_DIM] = value_t[:, lo:lo + PIECE].T
 
-    for load in loads:
-        load.wait()
     to_rows(o)
     y_part[0] = dot(rows_bf[1 - core], wo[...])
     y_copy = remote(y_part.at[0], y_recv, pair_send.at[0], pair_recv.at[0], partner)
@@ -438,50 +504,73 @@
     y_part[1] = dot(rows_bf[core], wo[...])
 
     dqt[...] = jnp.zeros(dqt.shape, F32)
-    both = (0, 1)
-    run(bwd_group, True, {
-        4: [(rs_far, '0x2'), (rs_far, '1y2'), (rs_far, '2z'), (rs_raw, '0x2'), (rs_raw, '1y2')],
-        6: [(rs_mid, '0x2'), (rs_mid, '1y2')],
-        8: [(rs_start, '0x3'), (rs_start, '1y3'), (rs_raw, '2z', (1,)), (rs_mid, '2z', (1,)),
-            (rs_fin, '0x2'), (rs_start, '0y2'), (rs_fin, '1y2'), (rs_start, '1x2')],
-        10: [(rs_mid, '0x3'), (rs_mid, '1y3'), (rs_mid, '0y2'), (rs_mid, '1x2')],
-        12: [(rs_start, '0x1'), (rs_start, '1y1'), (rs_raw, '2z', (0,)), (rs_mid, '2z', (0,)),
-             (rs_fin, '0y2'), (rs_fin, '1x2'), (rs_far, '0z'), (rs_far, '1z'),
-             (rs_fin, '0x3'), (rs_start, '0y3'), (rs_fin, '1y3'), (rs_start, '1x3')],
-        14: [(rs_mid, '0x1'), (rs_mid, '1y1'), (rs_mid, '0y3'), (rs_mid, '1x3')],
-    })
-    each(rs_start, '0x0', '1y0')
-    rs_fin('0x1')
-    rs_start('0y1')
-    rs_fin('1y1')
-    rs_start('1x1')
-    each(rs_fin, '0y3', '1x3')
-    for name in ('0z', '1z'):
-        rs_raw(name, (1,))
-        rs_mid(name, (1,))
-    y_copy.wait_recv()
-    y_out[...] = (y_part[1] + y_recv[...]).astype(BF)
-    to_rows((dqt[...] * scale).astype(BF))
-    dx_part[0] = dot_tb(rows_bf[1 - core], wq[...])
-    each(rs_mid, '0x0', '1y0', '0y1', '1x1')
-    rs_fin('2z')
-    rs_start('2x')
-    dx_part[1] = dot_tb(rows_bf[core], wq[...])
-    each(rs_fin, '0y1', '1x1')
-    for name in ('0z', '1z'):
-        rs_raw(name, (0,))
-        rs_mid(name, (0,))
-    rs_fin('0x0')
-    rs_start('0y0')
-    rs_fin('1y0')
-    rs_start('1x0')
-    rs_mid('2x')
-    each(rs_mid, '0y0', '1x0')
-    rs_fin('2x')
-    rs_start('2y')
-    each(rs_fin, '0y0', '1x0')
-    rs_mid('2y')
-    each(rs_fin, '0z', '1z', '2y')
+    plan = collections.defaultdict(list)
+
+    def at(time, rank_in_time, f, *args):
+        plan[time].append((rank_in_time, len(plan[time]), (f, *args)))
+
+    for p, o in enumerate((2, 3, 1, 0)):
+        for k, r in enumerate((2, 3, 1, 0)):
+            t = 4 * p + k + 1
+            sign = (1,) if k == 1 else (0,)
+            side = (1,) if p == 1 else (0,)
+            row = f'0x{o}{r}'
+            at(t, 0, rs_start, row)
+            at(t + 2, 1, rs_mid, row)
+            at(t + 4, 2, rs_fin, row)
+            if p == 0:
+                at(t, 0, rs_far, f'2z{r}')
+            elif p < 3:
+                at(t, 0, rs_raw, f'2z{r}', side)
+                at(t, 1, rs_mid, f'2z{r}', side)
+            else:
+                at(18, 2, rs_fin, f'2z{r}')
+            if k == 0:
+                at(t, 0, rs_far, f'1y{o}')
+                at(t + 4, 3, rs_far, f'0y{o}')
+            elif k < 3:
+                at(t, 0, rs_raw, f'1y{o}', sign)
+                at(t + 1, 1, rs_mid, f'1y{o}', sign)
+                at(t + 4, 3, rs_raw, f'0y{o}', sign)
+                at(t + 5, 1, rs_mid, f'0y{o}', sign)
+            else:
+                at(t + 3, 2, rs_fin, f'1y{o}')
+                at(t + 3, 3, rs_start, f'1x{o}')
+                at(t + 5, 1, rs_mid, f'1x{o}')
+                for late, name, last in ((6, '0z', f'0y{o}'), (7, '1z', f'1x{o}')):
+                    at(t + late, 2, rs_fin, last)
+                    if p == 0:
+                        at(t + late, 3, rs_far, name)
+                    elif p < 3:
+                        at(t + late, 3, rs_raw, name, side)
+                        at(21, 1, rs_mid, name, side)
+                    else:
+                        at(24, 2, rs_fin, name)
+    for name in ('3x', '4y'):
+        at(18, 3, rs_start, name)
+        at(20, 1, rs_mid, name)
+        at(21, 2, rs_fin, name)
+    for name in ('3y', '4x'):
+        at(21, 3, rs_start, name)
+        at(22, 1, rs_mid, name)
+        at(24, 2, rs_fin, name)
+    plan = {time: [op for _, _, op in sorted(ops, key=lambda e: e[:2])] for time, ops in sorted(plan.items())}
+    run(bwd_group, True, {time: ops for time, ops in plan.items() if time < 16})
+
+    def dx_start():
+        y_copy.wait_recv()
+        y_out[...] = (y_part[1] + y_recv[...]).astype(BF)
+        to_rows((dqt[...] * scale).astype(BF))
+        dx_part[0] = dot_tb(rows_bf[1 - core], wq[...])
+
+    for time, ops in plan.items():
+        if time >= 16:
+            for f, *args in ops:
+                f(*args)
+            if time == 16:
+                dx_start()
+            if time == 17:
+                dx_part[1] = dot_tb(rows_bf[core], wq[...])
 
     dk_own = dkv[me[0], me[1], me[2], 0:256, :].astype(BF)
     dv_own = dkv[me[0], me[1], me[2], 256:512, :].astype(BF)
@@ -504,7 +593,7 @@
     dx_copy.wait_send()
 
 
-def attention(qt, q, dot_t, do, kv_loc, w_query, w_key, w_value, w_out, groups):
+def attention(x_blk, dy_blk, w_query, w_key, w_value, w_out, groups):
     lanes = 2 * groups * PIECE
     dim = w_query.shape[0]
     vmem = pl.BlockSpec(memory_space=pltpu.VMEM)
@@ -513,9 +602,11 @@
     return pl.pallas_call(
         functools.partial(kernel, groups),
         out_shape=(jax.ShapeDtypeStruct((PIECE, dim), BF),) * 2,
-        in_specs=[vmem] * 5 + [anywhere] * 4,
+        in_specs=[anywhere] * 6,
         out_specs=(vmem,) * 2,
         scratch_shapes=[
+            pltpu.VMEM((2, *x_blk.shape), BF), pltpu.VMEM((2, *x_blk.shape), BF),
+            *[pltpu.VMEM(shape, BF) for shape in ((HEAD_DIM, lanes), (lanes, HEAD_DIM)) * 2],
             pltpu.VMEM((4, 4, 4, 512, HEAD_DIM), BF),
             pltpu.VMEM((4, 4, 4, 512, HEAD_DIM), F32),
             pltpu.VMEM((1, lanes), F32), pltpu.VMEM((1, lanes), F32),
@@ -525,15 +616,15 @@
             pltpu.VMEM((2, PIECE, groups * HEAD_DIM), BF),
             pltpu.VMEM((2, PIECE, dim), F32), pltpu.VMEM((PIECE, dim), F32),
             pltpu.VMEM((2, PIECE, dim), F32), pltpu.VMEM((PIECE, dim), F32),
-            pltpu.SemaphoreType.DMA((5,)),
-            pltpu.SemaphoreType.DMA((2,)), pltpu.SemaphoreType.DMA((2,)),
+            pltpu.SemaphoreType.DMA((6,)),
+            pltpu.SemaphoreType.DMA((4,)), pltpu.SemaphoreType.DMA((4,)),
             pltpu.SemaphoreType.DMA((len(AG_RINGS), 4)), pltpu.SemaphoreType.DMA((len(AG_RINGS), 4)),
             pltpu.SemaphoreType.DMA((len(RS_NAMES), 6)), pltpu.SemaphoreType.DMA((len(RS_NAMES), 6)),
             *rs_scratch(),
         ],
         compiler_params=pltpu.CompilerParams(collective_id=0, has_side_effects=True, vmem_limit_bytes=67043328),
         name='attention',
-    )(qt, q, dot_t, do, kv_loc, *weights)
+    )(x_blk, dy_blk, *weights)
 
 
 def solution(mesh):
@@ -541,17 +632,7 @@
 
     def local_step(x_blk, dy_blk, w_query, w_key, w_value, w_out):
         groups = w_query.shape[1] // HEAD_DIM
-        x_loc = lax.all_gather(x_blk, 'tp', axis=0, tiled=True)
-        dy_loc = lax.all_gather(dy_blk, 'tp', axis=0, tiled=True)
-
-        def fold(a):
-            return a.reshape(2, PIECE, groups, HEAD_DIM).transpose(0, 2, 1, 3).reshape(2 * groups * PIECE, HEAD_DIM)
-
-        q = fold(jnp.dot(x_loc, w_query, preferred_element_type=F32).astype(BF))
-        do = fold(dot_tb(dy_loc, w_out).astype(BF))
-        k = jnp.dot(x_loc, w_key, preferred_element_type=F32).astype(BF)
-        v = jnp.dot(x_loc, w_value, preferred_element_type=F32).astype(BF)
-        return attention(q.T, q, do.T, do, jnp.concatenate([k, v], axis=0), w_query, w_key, w_value, w_out, groups)
+        return attention(x_blk, dy_blk, w_query, w_key, w_value, w_out, groups)
 
     return jax.shard_map(local_step, mesh=mesh,
                          in_specs=(row_spec, row_spec, P(None, 'tp'), P(None, 'tp'), P(None, 'tp'), P('tp', None)),

time: 188 us -> 159 us (0.85)
  Pallas kernels: 167 us -> 154 us
  blocking collectives: 5.85 us -> 0 us
  matrix products: 4.57 us -> 0 us
  local copies, waits for them, and re-layouts: 7.57 us -> 3.53 us
    pallas_call x1, Pallas kernels: 167 us -> 154 us  [attention(): pl.pallas_call(functools.partial(kernel, groups), out_shape=(jax.ShapeDty...]
    all_gather x2 -> x0, blocking collectives: 5.85 us -> none  [the longest x1 3.49 us: local_step(): x_loc = lax.all_gather(x_blk, 'tp', axis=0, tiled=True)]
    dot_general x4 -> x0, matrix products: 4.57 us -> none  [the longest x1 1.98 us: local_step(): v = jnp.dot(x_loc, w_value, preferred_element_type=F32).astype(BF)]
    transpose x4 -> x0, local copies, waits for them, and re-layouts: 2.72 us -> none  [the longest x2 1.86 us: local_step(): return attention(q.T, q, do.T, do, jnp.concatenate([k, v], axis=0), w_que...]
    unnamed x14 -> x2, local copies, waits for them, and re-layouts: 4.32 us -> 3.53 us
where the time goes in v3:
time: 159 us
  Pallas kernels  154 us (97%)
  local copies, waits for them, and re-layouts  3.53 us (2%)
    pallas_call x1, Pallas kernels, attention(): pl.pallas_call(functools.partial(kernel, groups), out_shape=(jax.ShapeDty...  154 us
    unnamed x2, local copies, waits for them, and re-layouts  3.53 us

profile of v3, /device:TPU:1, one launch (start us, length us, event | category | flops | bytes accessed | tf_op | source)
XLA Modules:
  0.0 158.6 jit_solution(17232302228866287732)
XLA Ops:
  0.6 154.5 %attention.1 = (bf16[128,1536]{1,0:T(8,128)(2,1)}, bf16[128,1536]{1,0:T(8,128)(2,1)}) custom-call(bf16[128,1536]{1,0:T(8,128)(2,1)} %refs_0_.1, bf16[128,1536]{1,0:T(8,128)(2,1)} %refs_1_.1, bf16[1536,768]{1,0:T(8,128)(2,1)} %refs_2_.1, bf16[1536,128]{1,0:T(8,128)(2,1)} %refs_3_.1, bf16[1536,128]{1,0:T(8,128)(2,1)} %refs_4_.1, bf16[768,1536]{1,0:T(8,128)(2,1)} %refs_5_.1), custom_call_target="tpu_custom_call" | custom-call | tf_op jit(solution)/shard_map/attention/pallas_call | solution.py:602
  155.1 1.8 %copy.10 = bf16[128,1536]{1,0:T(8,128)(2,1)} copy(bf16[128,1536]{1,0:T(8,128)(2,1)} %get-tuple-element.4) | data formatting | bytes 786432
  156.9 1.8 %copy.11 = bf16[128,1536]{1,0:T(8,128)(2,1)} copy(bf16[128,1536]{1,0:T(8,128)(2,1)} %get-tuple-element.5) | data formatting | bytes 786432

commit v4 on v3

--- a/solution.py
+++ b/solution.py
@@ -19,20 +19,28 @@
 F32 = jnp.float32
 ALL = slice(None)
 
+BOTH = (0, 1)
+TORUS = (SIDE,) * 3
+BLOCK = 4 * PIECE
+KEY_A, KEY_B, VAL_A, VAL_B = (slice(n * PIECE, (n + 1) * PIECE) for n in range(SIDE))
+KEYS, VALUES = slice(0, 2 * PIECE), slice(2 * PIECE, BLOCK)
+SPIRAL = (0, 1, 3, 2)
+INWARD = (2, 3, 1, 0)
+
 AG_ROWS = ((0, 160), (160, 192), (352, 160))
 AG_HALF = (80, 96, 80)
 RS_ROWS = ((0, 160), (160, 160), (320, 192), (320, 96), (416, 96))
 RS_HALF = (80, 80, 96, 48, 48)
 STRIDE = (16, 4, 1)
-AG_RINGS = ('0a', '1a', '2a', '1c0') + tuple(n + str(o) for n in ('0b', '1b', '0r', '2b', '2c') for o in range(4)) + tuple(
-    n + str(o) for n in ('0c', '1c') for o in range(1, 4))
-RS_RINGS = {'0z': (0, 0, 0), '1z': (1, 0, 0), '3x': (3, 2, 1), '3y': (3, 1, 0), '4y': (4, 1, 1), '4x': (4, 2, 0)}
-for off in range(4):
+AG_RINGS = ('0a', '1a', '2a') + tuple(n + str(o) for n in ('0b', '1b', '0r', '2b', '2c', '0c', '1c') for o in range(SIDE))
+RS_RINGS = {'0z': (0, 0, 0), '1z': (1, 0, 0), '3y': (3, 1, 0), '4y': (4, 1, 1), '4x': (4, 2, 0)}
+for off in range(SIDE):
     RS_RINGS[f'2z{off}'] = (2, 0, 1)
     RS_RINGS[f'1y{off}'] = (1, 1, 1)
     RS_RINGS[f'0y{off}'] = (0, 1, 0)
     RS_RINGS[f'1x{off}'] = (1, 2, 0)
-    for row in range(4):
+    RS_RINGS[f'3x{off}'] = (3, 2, 0)
+    for row in range(SIDE):
         RS_RINGS[f'0x{off}{row}'] = (0, 2, 0)
 RS_NAMES = tuple(RS_RINGS)
 
@@ -64,7 +72,7 @@
      local_sem, pair_send, pair_recv, ag_send, ag_recv, rs_send, rs_recv, *rs_bufs) = refs
     rank = lax.axis_index('cp')
     core = lax.axis_index('tp')
-    me = (rank // 16, lax.rem(rank // 4, 4), lax.rem(rank, 4))
+    me = mz, my, mx = (rank // STRIDE[0], lax.rem(rank // SIDE, SIDE), lax.rem(rank, SIDE))
     width = groups * PIECE
     dqt = acc
 
@@ -103,23 +111,22 @@
 
     def ag_where(name):
         third = int(name[0])
-        z, y, x = me
         if name[1] == 'a':
-            return (third, 1, lambda q: (z, q, x)) if third == 2 else (third, 0, lambda q: (q, y, x))
+            return (third, 1, lambda q: (mz, q, mx)) if third == 2 else (third, 0, lambda q: (q, my, mx))
         off = int(name[2])
         if name[1] == 'r' or name[:2] == '2b':
             row = coord(1, off)
-            return third, 2, lambda q: (z, row, q)
+            return third, 2, lambda q: (mz, row, q)
         if third == 2:
             column = coord(2, off)
             return third, 0, lambda q: (q, ALL, column)
         plane = coord(0, off)
         if third == 0:
             if name[1] == 'b':
-                return third, 1, lambda q: (plane, q, x)
+                return third, 1, lambda q: (plane, q, mx)
             return third, 2, lambda q: (plane, ALL, q)
         if name[1] == 'b':
-            return third, 2, lambda q: (plane, y, q)
+            return third, 2, lambda q: (plane, my, q)
         return third, 1, lambda q: (plane, q, ALL)
 
     def ag_ref(name, off, rows):
@@ -138,34 +145,34 @@
 
     def direct(*names):
         for name in names:
-            for kind in (0, 1):
+            for kind in BOTH:
                 ag_push(name, kind, 0, AG_ROWS[int(name[0])])
 
     def relay(*names):
         for name in names:
             third = int(name[0])
-            for kind in (0, 1):
+            for kind in BOTH:
                 off = -1 if kind == 0 else 1
                 landed(ag_ref(name, off, AG_ROWS[third]), ag_recv.at[AG_RINGS.index(name), kind])
                 ag_push(name, 2 + kind, off, ag_split(third)[kind])
 
     def done(*names):
         for name in names:
-            for kind in (0, 1):
+            for kind in BOTH:
                 landed(ag_ref(name, 2, ag_split(int(name[0]))[kind]), ag_recv.at[AG_RINGS.index(name), 2 + kind])
 
     def rs_where(name):
-        z, y, x = me
         if name in ('0z', '1z'):
-            return lambda q: (q, y, x)
-        if name == '3x':
-            return lambda q: (z, ALL, q)
+            return lambda q: (q, my, mx)
+        if name[:2] == '3x':
+            row = coord(1, int(name[2]))
+            return lambda q: (mz, row, q)
         if name == '3y':
-            return lambda q: (z, q, x)
+            return lambda q: (mz, q, mx)
         if name == '4y':
-            return lambda q: (z, q, ALL)
+            return lambda q: (mz, q, ALL)
         if name == '4x':
-            return lambda q: (z, y, q)
+            return lambda q: (mz, my, q)
         if name[:2] == '2z':
             row = coord(1, int(name[2]))
             return lambda q: (q, row, ALL)
@@ -173,7 +180,7 @@
         if name[:2] == '0x':
             row = coord(1, int(name[3]))
             return lambda q: (plane, row, q)
-        return {'1y': lambda q: (plane, q, ALL), '0y': lambda q: (plane, q, x), '1x': lambda q: (plane, y, q)}[name[:2]]
+        return {'1y': lambda q: (plane, q, ALL), '0y': lambda q: (plane, q, mx), '1x': lambda q: (plane, my, q)}[name[:2]]
 
     def rs_split(part):
         start, size = RS_ROWS[part]
@@ -221,17 +228,17 @@
         else:
             one(0, 0)
 
-    def rs_far(name, signs=(0, 1)):
+    def rs_far(name, signs=BOTH):
         part, dim, _ = RS_RINGS[name]
         for sign in signs:
             rs_push(name, 0, sign, coord(dim, 2), rs_split(part)[sign])
 
-    def rs_raw(name, signs=(0, 1)):
+    def rs_raw(name, signs=BOTH):
         part, dim, _ = RS_RINGS[name]
         for sign in signs:
             rs_push(name, 1, sign, coord(dim, 1 if sign == 0 else -1), rs_split(part)[1 - sign])
 
-    def rs_mid(name, signs=(0, 1)):
+    def rs_mid(name, signs=BOTH):
         part, dim, _ = RS_RINGS[name]
         n = RS_NAMES.index(name)
         for sign in signs:
@@ -245,7 +252,7 @@
         part, dim, _ = RS_RINGS[name]
         n = RS_NAMES.index(name)
         for kind in (1, 2):
-            for sign in (0, 1):
+            for sign in BOTH:
                 rs_landed(name, kind, sign)
         rs_add(name, me[dim], RS_ROWS[part], [(rs_bufs[2 * n + 1].at[0], 0), (rs_bufs[2 * n + 1].at[1], 0)])
 
@@ -299,8 +306,8 @@
         return dot(ds, q_ref[ql, :]) * scale, dot(pb, do_ref[ql, :])
 
     def group_loop(zp, yp, body):
-        here = zp * 4 + yp
-        mine = me[0] * 4 + me[1]
+        here = zp * SIDE + yp
+        mine = mz * SIDE + my
         mixed = here == mine
         high = here > mine
         count = jnp.where(mixed, 3, 2)
@@ -312,18 +319,18 @@
 
             @pl.when(high)
             def _():
-                kt[...] = kv[zp, yp, pl.ds(2 * u, 2), 0:256, :].reshape(512, HEAD_DIM)
-                vt[...] = kv[zp, yp, pl.ds(2 * u, 2), 256:512, :].reshape(512, HEAD_DIM)
+                kt[...] = kv[zp, yp, pl.ds(2 * u, 2), KEYS, :].reshape(BLOCK, HEAD_DIM)
+                vt[...] = kv[zp, yp, pl.ds(2 * u, 2), VALUES, :].reshape(BLOCK, HEAD_DIM)
 
             @pl.when(jnp.logical_and(jnp.logical_not(high), jnp.logical_not(second)))
             def _():
-                kt[...] = kv[zp, yp, :, 0:128, :].reshape(512, HEAD_DIM)
-                vt[...] = kv[zp, yp, :, 256:384, :].reshape(512, HEAD_DIM)
+                kt[...] = kv[zp, yp, :, KEY_A, :].reshape(BLOCK, HEAD_DIM)
+                vt[...] = kv[zp, yp, :, VAL_A, :].reshape(BLOCK, HEAD_DIM)
 
             @pl.when(second)
             def _():
-                kt[...] = kv[zp, yp, :, 128:256, :].reshape(512, HEAD_DIM)
-                vt[...] = kv[zp, yp, :, 384:512, :].reshape(512, HEAD_DIM)
+                kt[...] = kv[zp, yp, :, KEY_B, :].reshape(BLOCK, HEAD_DIM)
+                vt[...] = kv[zp, yp, :, VAL_B, :].reshape(BLOCK, HEAD_DIM)
 
             body(u, here * 4, second, high, half, masked)
             return carry
@@ -331,14 +338,14 @@
         lax.fori_loop(0, count, step, 0)
 
     def fwd_group(zp, yp):
-        here = zp * 4 + yp
-        mine = me[0] * 4 + me[1]
+        here = zp * SIDE + yp
+        mine = mz * SIDE + my
         first, last = slice(0, width), slice(width, 2 * width)
 
         @pl.when(here < mine)
         def _():
-            k = kv[zp, yp, :, 0:128, :].reshape(512, HEAD_DIM)
-            v = kv[zp, yp, :, 256:384, :].reshape(512, HEAD_DIM)
+            k = kv[zp, yp, :, KEY_A, :].reshape(BLOCK, HEAD_DIM)
+            v = kv[zp, yp, :, VAL_A, :].reshape(BLOCK, HEAD_DIM)
             s0, s1 = scores(k, first), scores(k, last)
             online(s0, v, first)
             online(s1, v, last)
@@ -346,9 +353,9 @@
         @pl.when(here > mine)
         def _():
             pairs = (slice(0, 2), slice(2, 4))
-            s0, s1 = (scores(kv[zp, yp, pair, 0:256, :].reshape(512, HEAD_DIM), last) for pair in pairs)
+            s0, s1 = (scores(kv[zp, yp, pair, KEYS, :].reshape(BLOCK, HEAD_DIM), last) for pair in pairs)
             for s, pair in zip((s0, s1), pairs):
-                online(s, kv[zp, yp, pair, 256:512, :].reshape(512, HEAD_DIM), last)
+                online(s, kv[zp, yp, pair, VALUES, :].reshape(BLOCK, HEAD_DIM), last)
 
         def body(u, j0, second, high, half, masked):
             ql = lanes_of(half)
@@ -361,18 +368,18 @@
 
     def bwd_group(zp, yp):
         def first(dk, dv):
-            none = jnp.zeros((SIDE, 128, HEAD_DIM), F32)
-            dkv[zp, yp, :, 0:128, :] = dk.reshape(4, 128, HEAD_DIM)
-            dkv[zp, yp, :, 128:256, :] = none
-            dkv[zp, yp, :, 256:384, :] = dv.reshape(4, 128, HEAD_DIM)
-            dkv[zp, yp, :, 384:512, :] = none
+            none = jnp.zeros((SIDE, PIECE, HEAD_DIM), F32)
+            dkv[zp, yp, :, KEY_A, :] = dk.reshape(SIDE, PIECE, HEAD_DIM)
+            dkv[zp, yp, :, KEY_B, :] = none
+            dkv[zp, yp, :, VAL_A, :] = dv.reshape(SIDE, PIECE, HEAD_DIM)
+            dkv[zp, yp, :, VAL_B, :] = none
 
         def body(u, j0, second, high, half, masked):
             def keep(dk, dv):
                 @pl.when(high)
                 def _():
-                    dkv[zp, yp, pl.ds(2 * u, 2), 0:256, :] = dk.reshape(2, 256, HEAD_DIM)
-                    dkv[zp, yp, pl.ds(2 * u, 2), 256:512, :] = dv.reshape(2, 256, HEAD_DIM)
+                    dkv[zp, yp, pl.ds(2 * u, 2), KEYS, :] = dk.reshape(2, 2 * PIECE, HEAD_DIM)
+                    dkv[zp, yp, pl.ds(2 * u, 2), VALUES, :] = dv.reshape(2, 2 * PIECE, HEAD_DIM)
 
                 @pl.when(jnp.logical_and(jnp.logical_not(high), u == 0))
                 def _():
@@ -380,8 +387,8 @@
 
                 @pl.when(jnp.logical_and(jnp.logical_not(high), u != 0))
                 def _():
-                    dkv[zp, yp, :, 0:128, :] += dk.reshape(4, 128, HEAD_DIM)
-                    dkv[zp, yp, :, 256:384, :] += dv.reshape(4, 128, HEAD_DIM)
+                    dkv[zp, yp, :, KEY_A, :] += dk.reshape(SIDE, PIECE, HEAD_DIM)
+                    dkv[zp, yp, :, VAL_A, :] += dv.reshape(SIDE, PIECE, HEAD_DIM)
 
             @pl.when(jnp.logical_not(masked))
             def _():
@@ -393,8 +400,8 @@
 
                 @pl.when(second)
                 def _():
-                    dkv[zp, yp, :, 128:256, :] = dk.reshape(4, 128, HEAD_DIM)
-                    dkv[zp, yp, :, 384:512, :] = dv.reshape(4, 128, HEAD_DIM)
+                    dkv[zp, yp, :, KEY_B, :] = dk.reshape(SIDE, PIECE, HEAD_DIM)
+                    dkv[zp, yp, :, VAL_B, :] = dv.reshape(SIDE, PIECE, HEAD_DIM)
 
                 @pl.when(jnp.logical_not(second))
                 def _():
@@ -415,7 +422,7 @@
             d, r = g // 4, lax.rem(g, 4)
             if reverse:
                 d, r = 3 - d, 3 - r
-            compute(lax.rem(me[0] + spiral(d), SIDE), lax.rem(me[1] + spiral(r), SIDE))
+            compute(lax.rem(mz + spiral(d), SIDE), lax.rem(my + spiral(r), SIDE))
             return carry
 
         lax.fori_loop(0, 16, step, 0)
@@ -432,8 +439,8 @@
     def project_kv(slot):
         rows = xs[slot]
         lo = pl.multiple_of(slot * PIECE, PIECE)
-        kv[me[0], me[1], me[2], pl.ds(lo, PIECE), :] = dot(rows, wk[...]).astype(BF)
-        kv[me[0], me[1], me[2], pl.ds(256 + lo, PIECE), :] = dot(rows, wv[...]).astype(BF)
+        kv[*me, pl.ds(lo, PIECE), :] = dot(rows, wk[...]).astype(BF)
+        kv[*me, pl.ds(256 + lo, PIECE), :] = dot(rows, wv[...]).astype(BF)
 
     def spread(rows, slot, flat, flat_t):
         for h in range(groups):
@@ -460,27 +467,29 @@
     relay('1b0', '0r0', '0b0', '2a', '2b0')
     direct('0r1', '0r3', '2b1', '2b3')
     project_q(1 - core)
+    relay('0a', '1a')
+    direct('0b1', '1b1', '0b3', '1b3')
     done('1b0')
     direct('1c0')
-    relay('0a', '1a')
-    direct('0b1', '1b1', '0b3', '1b3')
     done('0b0')
     direct('0r2')
     done('2a')
     direct('2b2', '2c0')
     done('0r0', '2b0')
     run(fwd_group, False, {
-        1: [(relay, '0r1', '2b1', '0r3', '2b3', '1c0'), (loads['wo'].wait,), (project_do, core),
-            (relay, '0b1', '1b1', '0b3', '1b3'), (done, '0r1', '2b1')],
-        2: [(relay, '0r2', '2b2'), (direct, '2c1', '2c3'), (done, '0b1'), (direct, '0c1'), (done, '1b1'), (direct, '1c1'),
-            (done, '0b3'), (direct, '0c3'), (done, '1b3'), (direct, '1c3'), (done, '0r3', '2b3')],
-        3: [(relay, '2c0'), (done, '0a', '1a'), (direct, '0b2', '1b2'), (done, '0r2', '2b2', '1c0'), (direct, '2c2'),
-            (landed, dys.at[1 - core], pair_recv.at[3]), (project_do, 1 - core), (relay, '0c1', '1c1')],
+        1: [(relay, '0b1', '1b1', '0b3', '1b3'), (done, '0a', '1a'), (direct, '0b2', '1b2'),
+            (relay, '0r1', '2b1', '0r3', '2b3', '2b2'), (direct, '2c1', '2c3'), (relay, '1c0'),
+            (done, '0b1'), (direct, '0c1'), (done, '1b1'), (direct, '1c1'),
+            (loads['wo'].wait,), (project_do, core), (done, '0r1', '2b1')],
+        2: [(relay, '0r2'), (done, '2b3', '2b2'), (direct, '2c2'),
+            (done, '0b3'), (direct, '0c3'), (done, '1b3'), (direct, '1c3'), (relay, '0b2', '1b2'), (done, '0r3')],
+        3: [(relay, '2c0'), (done, '0r2', '1c0'),
+            (landed, dys.at[1 - core], pair_recv.at[3]), (project_do, 1 - core), (relay, '0c1', '1c1'),
+            (done, '0b2', '1b2'), (direct, '0c2', '1c2')],
         4: [(relay, '2c1', '2c3', '2c2'), (done, '0c1', '1c1')],
-        5: [(relay, '0c3', '1c3'), (relay, '0b2', '1b2')],
-        7: [(done, '0b2', '1b2'), (direct, '0c2', '1c2')],
+        5: [(relay, '0c3', '1c3')],
+        7: [(relay, '0c2', '1c2')],
         8: [(done, '0c3', '1c3')],
-        10: [(relay, '0c2', '1c2')],
         12: [(done, '0c2', '1c2', '2c0', '2c1', '2c2', '2c3')],
     })
     x_copy.wait_send()
@@ -498,10 +507,7 @@
                 rows_bf[s, :, h * HEAD_DIM:(h + 1) * HEAD_DIM] = value_t[:, lo:lo + PIECE].T
 
     to_rows(o)
-    y_part[0] = dot(rows_bf[1 - core], wo[...])
     y_copy = remote(y_part.at[0], y_recv, pair_send.at[0], pair_recv.at[0], partner)
-    y_copy.start()
-    y_part[1] = dot(rows_bf[core], wo[...])
 
     dqt[...] = jnp.zeros(dqt.shape, F32)
     plan = collections.defaultdict(list)
@@ -509,11 +515,12 @@
     def at(time, rank_in_time, f, *args):
         plan[time].append((rank_in_time, len(plan[time]), (f, *args)))
 
-    for p, o in enumerate((2, 3, 1, 0)):
-        for k, r in enumerate((2, 3, 1, 0)):
-            t = 4 * p + k + 1
-            sign = (1,) if k == 1 else (0,)
-            side = (1,) if p == 1 else (0,)
+    low, up = (1,), (0,)
+    for p, o in enumerate(INWARD):
+        for k, r in enumerate(INWARD):
+            t = SIDE * p + k + 1
+            sign = low if k == 1 else up
+            side = low if p == 1 else up
             row = f'0x{o}{r}'
             at(t, 0, rs_start, row)
             at(t + 2, 1, rs_mid, row)
@@ -523,8 +530,6 @@
             elif p < 3:
                 at(t, 0, rs_raw, f'2z{r}', side)
                 at(t, 1, rs_mid, f'2z{r}', side)
-            else:
-                at(18, 2, rs_fin, f'2z{r}')
             if k == 0:
                 at(t, 0, rs_far, f'1y{o}')
                 at(t + 4, 3, rs_far, f'0y{o}')
@@ -546,20 +551,31 @@
                         at(21, 1, rs_mid, name, side)
                     else:
                         at(24, 2, rs_fin, name)
-    for name in ('3x', '4y'):
-        at(18, 3, rs_start, name)
-        at(20, 1, rs_mid, name)
-        at(21, 2, rs_fin, name)
+    for t, r, f, more in ((15, 2, rs_far, None), (17, 3, rs_raw, low), (18, 1, rs_raw, up), (19, 0, None, None)):
+        at(t, 4, rs_fin, f'2z{r}')
+        at(t, 5, rs_start, f'3x{r}')
+        at(t + 2, 1, rs_mid, f'3x{r}')
+        at(t + 3, 2, rs_fin, f'3x{r}')
+        if f is None:
+            at(20, 2, rs_fin, '4y')
+            at(20, 2, rs_start, '4x')
+            at(21, 1, rs_mid, '4x')
+        else:
+            for start, name, rank_in_time in ((t, '4y', 5), (t + 3, '3y', 2)):
+                if more is None:
+                    at(start, rank_in_time, f, name)
+                else:
+                    at(start, rank_in_time, f, name, more)
+                    at(start + 1, 0, rs_mid, name, more)
     for name in ('3y', '4x'):
-        at(21, 3, rs_start, name)
-        at(22, 1, rs_mid, name)
-        at(24, 2, rs_fin, name)
+        at(23, 2, rs_fin, name)
     plan = {time: [op for _, _, op in sorted(ops, key=lambda e: e[:2])] for time, ops in sorted(plan.items())}
     run(bwd_group, True, {time: ops for time, ops in plan.items() if time < 16})
 
     def dx_start():
-        y_copy.wait_recv()
-        y_out[...] = (y_part[1] + y_recv[...]).astype(BF)
+        y_part[0] = dot(rows_bf[1 - core], wo[...])
+        y_copy.start()
+        y_part[1] = dot(rows_bf[core], wo[...])
         to_rows((dqt[...] * scale).astype(BF))
         dx_part[0] = dot_tb(rows_bf[1 - core], wq[...])
 
@@ -571,9 +587,11 @@
                 dx_start()
             if time == 17:
                 dx_part[1] = dot_tb(rows_bf[core], wq[...])
-
-    dk_own = dkv[me[0], me[1], me[2], 0:256, :].astype(BF)
-    dv_own = dkv[me[0], me[1], me[2], 256:512, :].astype(BF)
+                y_copy.wait_recv()
+                y_out[...] = (y_part[1] + y_recv[...]).astype(BF)
+
+    dk_own = dkv[*me, KEYS, :].astype(BF)
+    dv_own = dkv[*me, VALUES, :].astype(BF)
     kt[0:256, :] = dk_own
     vt[0:256, :] = dv_own
 
@@ -607,11 +625,11 @@
         scratch_shapes=[
             pltpu.VMEM((2, *x_blk.shape), BF), pltpu.VMEM((2, *x_blk.shape), BF),
             *[pltpu.VMEM(shape, BF) for shape in ((HEAD_DIM, lanes), (lanes, HEAD_DIM)) * 2],
-            pltpu.VMEM((4, 4, 4, 512, HEAD_DIM), BF),
-            pltpu.VMEM((4, 4, 4, 512, HEAD_DIM), F32),
+            pltpu.VMEM((*TORUS, BLOCK, HEAD_DIM), BF),
+            pltpu.VMEM((*TORUS, BLOCK, HEAD_DIM), F32),
             pltpu.VMEM((1, lanes), F32), pltpu.VMEM((1, lanes), F32),
             pltpu.VMEM((HEAD_DIM, lanes), F32), pltpu.VMEM((1, lanes), F32),
-            pltpu.VMEM((512, HEAD_DIM), BF), pltpu.VMEM((512, HEAD_DIM), BF),
+            pltpu.VMEM((BLOCK, HEAD_DIM), BF), pltpu.VMEM((BLOCK, HEAD_DIM), BF),
             *[pltpu.VMEM(w.shape, BF) for w in weights],
             pltpu.VMEM((2, PIECE, groups * HEAD_DIM), BF),
             pltpu.VMEM((2, PIECE, dim), F32), pltpu.VMEM((PIECE, dim), F32),
@@ -627,12 +645,22 @@
     )(x_blk, dy_blk, *weights)
 
 
+def handover(y, dx):
+    def body(y_in, dx_in, y_end, dx_end):
+        y_end[...] = y_in[...]
+        dx_end[...] = dx_in[...]
+
+    vmem = pl.BlockSpec(memory_space=pltpu.VMEM)
+    shape = jax.ShapeDtypeStruct(y.shape, y.dtype)
+    return pl.pallas_call(body, out_shape=(shape, shape), in_specs=[vmem] * 2, out_specs=(vmem,) * 2, name='handover')(y, dx)
+
+
 def solution(mesh):
     row_spec = P(('dp', 'cp', 'tp'), None)
 
     def local_step(x_blk, dy_blk, w_query, w_key, w_value, w_out):
         groups = w_query.shape[1] // HEAD_DIM
-        return attention(x_blk, dy_blk, w_query, w_key, w_value, w_out, groups)
+        return handover(*attention(x_blk, dy_blk, w_query, w_key, w_value, w_out, groups))
 
     return jax.shard_map(local_step, mesh=mesh,
                          in_specs=(row_spec, row_spec, P(None, 'tp'), P(None, 'tp'), P(None, 'tp'), P('tp', None)),

time: 159 us -> 147 us (0.925)
  Pallas kernels: 154 us -> 146 us
  local copies, waits for them, and re-layouts: 3.53 us -> 0 us
    pallas_call x1, Pallas kernels: 154 us -> 144 us  [attention(): pl.pallas_call(functools.partial(kernel, groups), out_shape=(jax.ShapeDty...]
    unnamed x2 -> x0, local copies, waits for them, and re-layouts: 3.53 us -> none
    pallas_call x0 -> x1, Pallas kernels: none -> 2.02 us  [handover(): pl.pallas_call(body, out_shape=(shape, shape), in_specs=[vmem] * 2, out_s...]
where the time goes in v4:
time: 147 us
  Pallas kernels  146 us (99%)
    pallas_call x1, Pallas kernels, attention(): pl.pallas_call(functools.partial(kernel, groups), out_shape=(jax.ShapeDty...  144 us

profile of v4, /device:TPU:1, one launch (start us, length us, event | category | flops | bytes accessed | tf_op | source)
XLA Modules:
  0.0 146.9 jit_solution(46376524443801849)
XLA Ops:
  0.6 144.2 %attention.1 = (bf16[128,1536]{1,0:T(8,128)(2,1)}, bf16[128,1536]{1,0:T(8,128)(2,1)}) custom-call(bf16[128,1536]{1,0:T(8,128)(2,1)} %refs_0_.1, bf16[128,1536]{1,0:T(8,128)(2,1)} %refs_1_.1, bf16[1536,768]{1,0:T(8,128)(2,1)} %refs_2_.1, bf16[1536,128]{1,0:T(8,128)(2,1)} %refs_3_.1, bf16[1536,128]{1,0:T(8,128)(2,1)} %refs_4_.1, bf16[768,1536]{1,0:T(8,128)(2,1)} %refs_5_.1), custom_call_target="tpu_custom_call" | custom-call | tf_op jit(solution)/shard_map/attention/pallas_call | solution.py:620
  144.9 2.0 %handover.1 = (bf16[128,1536]{1,0:T(8,128)(2,1)}, bf16[128,1536]{1,0:T(8,128)(2,1)}) custom-call(bf16[128,1536]{1,0:T(8,128)(2,1)} %get-tuple-element.4.y_in, bf16[128,1536]{1,0:T(8,128)(2,1)} %get-tuple-element.5.dx_in), custom_call_target="tpu_custom_call" | custom-call | tf_op jit(solution)/shard_map/handover/pallas_call | solution.py:655

commit v5 on v4

--- a/solution.py
+++ b/solution.py
@@ -337,25 +337,33 @@
 
         lax.fori_loop(0, count, step, 0)
 
+    def chunks(lo, hi):
+        return [slice(n, n + 384) for n in range(lo, hi, 384)]
+
+    def stream(work):
+        held = [scores(k, ql) for k, _, ql in work[:1]]
+        for n, (_, v, ql) in enumerate(work):
+            if n + 1 < len(work):
+                k, _, later = work[n + 1]
+                held.append(scores(k, later))
+            online(held.pop(0), v, ql)
+
     def fwd_group(zp, yp):
         here = zp * SIDE + yp
         mine = mz * SIDE + my
-        first, last = slice(0, width), slice(width, 2 * width)
 
         @pl.when(here < mine)
         def _():
             k = kv[zp, yp, :, KEY_A, :].reshape(BLOCK, HEAD_DIM)
             v = kv[zp, yp, :, VAL_A, :].reshape(BLOCK, HEAD_DIM)
-            s0, s1 = scores(k, first), scores(k, last)
-            online(s0, v, first)
-            online(s1, v, last)
+            stream([(k, v, ql) for ql in chunks(0, 2 * width)])
 
         @pl.when(here > mine)
         def _():
             pairs = (slice(0, 2), slice(2, 4))
-            s0, s1 = (scores(kv[zp, yp, pair, KEYS, :].reshape(BLOCK, HEAD_DIM), last) for pair in pairs)
-            for s, pair in zip((s0, s1), pairs):
-                online(s, kv[zp, yp, pair, VALUES, :].reshape(BLOCK, HEAD_DIM), last)
+            work = [(kv[zp, yp, pair, KEYS, :].reshape(BLOCK, HEAD_DIM), kv[zp, yp, pair, VALUES, :].reshape(BLOCK, HEAD_DIM))
+                    for pair in pairs]
+            stream([(k, v, ql) for k, v in work for ql in chunks(width, 2 * width)])
 
         def body(u, j0, second, high, half, masked):
             ql = lanes_of(half)
@@ -484,9 +492,8 @@
         2: [(relay, '0r2'), (done, '2b3', '2b2'), (direct, '2c2'),
             (done, '0b3'), (direct, '0c3'), (done, '1b3'), (direct, '1c3'), (relay, '0b2', '1b2'), (done, '0r3')],
         3: [(relay, '2c0'), (done, '0r2', '1c0'),
-            (landed, dys.at[1 - core], pair_recv.at[3]), (project_do, 1 - core), (relay, '0c1', '1c1'),
-            (done, '0b2', '1b2'), (direct, '0c2', '1c2')],
-        4: [(relay, '2c1', '2c3', '2c2'), (done, '0c1', '1c1')],
+            (landed, dys.at[1 - core], pair_recv.at[3]), (project_do, 1 - core), (relay, '0c1', '1c1')],
+        4: [(relay, '2c1', '2c3', '2c2'), (done, '0b2', '1b2'), (direct, '0c2', '1c2'), (done, '0c1', '1c1')],
         5: [(relay, '0c3', '1c3')],
         7: [(relay, '0c2', '1c2')],
         8: [(done, '0c3', '1c3')],

time: 147 us -> 146 us (level)
  no operation moved by 1% of the time
where the time goes in v5:
time: 146 us; the launch traced here: 145 us
  Pallas kernels  145 us (99%)
    pallas_call x1, Pallas kernels, attention(): pl.pallas_call(functools.partial(kernel, groups), out_shape=(jax.ShapeDty...  143 us

profile of v5, /device:TPU:1, one launch (start us, length us, event | category | flops | bytes accessed | tf_op | source)
XLA Modules:
  0.0 145.4 jit_solution(796663093736503444)
XLA Ops:
  0.6 142.8 %attention.1 = (bf16[128,1536]{1,0:T(8,128)(2,1)}, bf16[128,1536]{1,0:T(8,128)(2,1)}) custom-call(bf16[128,1536]{1,0:T(8,128)(2,1)} %refs_0_.1, bf16[128,1536]{1,0:T(8,128)(2,1)} %refs_1_.1, bf16[1536,768]{1,0:T(8,128)(2,1)} %refs_2_.1, bf16[1536,128]{1,0:T(8,128)(2,1)} %refs_3_.1, bf16[1536,128]{1,0:T(8,128)(2,1)} %refs_4_.1, bf16[768,1536]{1,0:T(8,128)(2,1)} %refs_5_.1), custom_call_target="tpu_custom_call" | custom-call | tf_op jit(solution)/shard_map/attention/pallas_call | solution.py:627
  143.4 2.0 %handover.1 = (bf16[128,1536]{1,0:T(8,128)(2,1)}, bf16[128,1536]{1,0:T(8,128)(2,1)}) custom-call(bf16[128,1536]{1,0:T(8,128)(2,1)} %get-tuple-element.4.y_in, bf16[128,1536]{1,0:T(8,128)(2,1)} %get-tuple-element.5.dx_in), custom_call_target="tpu_custom_call" | custom-call | tf_op jit(solution)/shard_map/handover/pallas_call | solution.py:662
